TPU v7x, 64 devices: a 2x2x8 block of a 4x4x8 slice. The times are simulated.
64 devices in a mesh: dp: 4 (over x, y), sp: 16 (over z, core).
Axes of the slice: x: 2, y: 2, z: 8, core: 2. Of those that a mesh axis runs over, the one named last changes fastest.
The devices are a block of a 4x4x8 slice.
Arguments:
- hidden: bfloat16 [192, 4096], P('dp'), parts along dimension 0
- ln_gamma: float32 [4096], replicated
- ln_beta: float32 [4096], replicated
- w_qkv: bfloat16 [4096, 4608], replicated
- w_out: bfloat16 [4096, 4096], replicated
- w_up: bfloat16 [4096, 16384], P(None, 'sp')
- w_down: bfloat16 [16384, 4096], P('sp')
- k_cache: bfloat16 [192, 2048, 256], P('dp', 'sp'), parts along dimension 0
- v_cache: bfloat16 [192, 2048, 256], P('dp', 'sp'), parts along dimension 0
- positions: int32 [192], P('dp'), parts along dimension 0
Outputs:
- output 1: bfloat16 [192, 4096], P('dp'), parts along dimension 0
- output 2: bfloat16 [192, 2048, 256], P('dp', 'sp'), parts along dimension 0
- output 3: bfloat16 [192, 2048, 256], P('dp', 'sp'), parts along dimension 0
There are 4 independent parts. A program takes and returns all parts, laid end to end along the dimension named above; an argument that names none is the same for every part.
All inputs are finite; a program needn't handle non-finite values.
Results may differ from a plain program's by a relative error of at most 0.00517107.
Values sent between devices are 32-bit elements.
A program may use at most 768 MiB of HBM per device.

v0:
```python
import jax
import jax.numpy as jnp
from jax import lax
from jax.sharding import PartitionSpec as P

LN_EPS = 1e-5
ROPE_BASE = 10000.0
NEG_FILL = -1e30


def layer_norm(hidden, ln_gamma, ln_beta):
    hidden_f32 = hidden.astype(jnp.float32)
    row_mean = jnp.mean(hidden_f32, axis=-1, keepdims=True)
    centered = hidden_f32 - row_mean
    row_var = jnp.mean(centered * centered, axis=-1, keepdims=True)
    return (centered * lax.rsqrt(row_var + LN_EPS) * ln_gamma + ln_beta).astype(jnp.bfloat16)


def rotary_tables(positions, head_dim):
    inv_freq = 1.0 / (ROPE_BASE ** (jnp.arange(0, head_dim, 2, dtype=jnp.float32) / head_dim))
    angles = positions.astype(jnp.float32)[:, None] * inv_freq[None, :]
    cos_half = jnp.cos(angles)
    sin_half = jnp.sin(angles)
    return jnp.concatenate([cos_half, cos_half], axis=-1), jnp.concatenate([sin_half, sin_half], axis=-1)


def apply_rotary(vecs, cos_full, sin_full):
    vecs_f32 = vecs.astype(jnp.float32)
    half_dim = vecs.shape[-1] // 2
    rotated = jnp.concatenate([-vecs_f32[..., half_dim:], vecs_f32[..., :half_dim]], axis=-1)
    return (vecs_f32 * cos_full + rotated * sin_full).astype(jnp.bfloat16)


def local_stats(q_rot, k_block, v_block, local_pos):
    head_dim = q_rot.shape[-1]
    slot_ids = jnp.arange(k_block.shape[1])
    scores = jnp.einsum('bhd,bsd->bhs', q_rot, k_block, preferred_element_type=jnp.float32) * head_dim ** -0.5
    valid_mask = (slot_ids[None, :] <= local_pos[:, None])[:, None, :]
    masked = jnp.where(valid_mask, scores, NEG_FILL)
    block_max = jnp.max(masked, axis=-1)
    exp_scores = jnp.where(valid_mask, jnp.exp(masked - block_max[..., None]), 0.0)
    block_sum = jnp.sum(exp_scores, axis=-1)
    block_ctx = jnp.einsum('bhs,bsd->bhd', exp_scores.astype(jnp.bfloat16), v_block, preferred_element_type=jnp.float32)
    return jnp.concatenate([block_ctx, block_max[..., None], block_sum[..., None]], axis=-1)


def combine_stats(all_stats):
    head_dim = all_stats.shape[-1] - 2
    block_max = all_stats[..., head_dim]
    top_max = jnp.max(block_max, axis=0)
    scale_w = jnp.exp(block_max - top_max[None])
    total_sum = jnp.sum(all_stats[..., head_dim + 1] * scale_w, axis=0)
    total_ctx = jnp.sum(all_stats[..., :head_dim] * scale_w[..., None], axis=0)
    return (total_ctx / total_sum[..., None]).astype(jnp.bfloat16)


def device_step(hidden, ln_gamma, ln_beta, w_qkv, w_out, w_up, w_down, k_cache, v_cache, positions):
    batch_rows = hidden.shape[0]
    seq_dev, head_dim = k_cache.shape[1], k_cache.shape[2]
    num_heads = w_out.shape[0] // head_dim
    normed = layer_norm(hidden, ln_gamma, ln_beta)
    qkv_proj = jnp.dot(normed, w_qkv, preferred_element_type=jnp.float32).astype(jnp.bfloat16)
    qkv_proj = qkv_proj.reshape(batch_rows, num_heads + 2, head_dim)
    cos_full, sin_full = rotary_tables(positions, head_dim)
    q_rot = apply_rotary(qkv_proj[:, :num_heads], cos_full[:, None, :], sin_full[:, None, :])
    k_rot = apply_rotary(qkv_proj[:, num_heads], cos_full, sin_full)
    v_new = qkv_proj[:, num_heads + 1]
    local_pos = positions - lax.axis_index('sp') * seq_dev
    write_mask = (jnp.arange(seq_dev)[None, :] == local_pos[:, None])[:, :, None]
    k_next = jnp.where(write_mask, k_rot[:, None, :], k_cache)
    v_next = jnp.where(write_mask, v_new[:, None, :], v_cache)
    block_stats = local_stats(q_rot, k_next, v_next, local_pos)
    all_stats = lax.all_gather(block_stats, 'sp')
    context = combine_stats(all_stats).reshape(batch_rows, num_heads * head_dim)
    attn_out = jnp.dot(context, w_out, preferred_element_type=jnp.float32)
    up_proj = jnp.dot(normed, w_up, preferred_element_type=jnp.float32)
    activated = jax.nn.gelu(up_proj, approximate=False).astype(jnp.bfloat16)
    mlp_part = jnp.dot(activated, w_down, preferred_element_type=jnp.float32)
    mlp_out = lax.psum(mlp_part, 'sp')
    out_hidden = (hidden.astype(jnp.float32) + attn_out + mlp_out).astype(jnp.bfloat16)
    return out_hidden, k_next, v_next


def solution(mesh):
    cache_spec = P('dp', 'sp', None)
    in_specs = (P('dp', None), P(None), P(None), P(None, None), P(None, None), P(None, 'sp'), P('sp', None), cache_spec, cache_spec, P('dp'))
    out_specs = (P('dp', None), cache_spec, cache_spec)
    return jax.shard_map(device_step, mesh=mesh, in_specs=in_specs, out_specs=out_specs, check_vma=False)
```

profile of v0, /device:TPU:21, one launch (start us, length us, event | category | flops | bytes accessed | tf_op | source)
XLA Modules:
  0.0 277.2 jit_solution(8902787659032569156)
XLA Ops:
  7.2 0.1 all-gather.3.cloned.1.call-start
  7.3 0.7 fusion.113
  8.0 0.2 multiply_cosine_fusion
  8.2 0.2 multiply_cosine_fusion.1
  8.3 1.2 convert_reduce_fusion
  9.5 0.0 copy-start.7
  9.5 1.3 fusion.6
  10.8 0.0 copy-done.7
  10.8 0.0 copy-start.8
  10.8 0.5 copy-done.8
  11.3 15.4 %convolution_convert_fusion = bf16[48,4608]{1,0:T(8,128)(2,1)S(1)} fusion(bf16[4096,4608]{1,0:T(8,128)(2,1)} %param.13, bf16[48,4096]{1,0:T(8,128)(2,1)} %param.10, f32[4096]{0:T(1024)} %param.12, f32[4096]{0:T(1024)} %param.11, f32[48]{0:T(128)S(1)} %add_rsqrt_fusion, f32[48]{0:T(128)S(1)} %broadcast_multiply_fusion), kind=kOutput, calls=%fused_computation.2 | convolution fusion | flops 1813340160 | bytes 38617472 | tf_op jit(solution)/shard_map/dot_general | solution.py:62
  26.7 0.2 reshape.199
  26.9 0.0 copy-start.3
  26.9 0.1 fusion.112
  27.0 0.1 slice_convert_fusion
  27.1 0.1 iota_compare_fusion.1
  27.2 0.1 slice_negate_fusion
  27.3 0.4 copy-done.3
  27.7 4.0 %broadcast_select_fusion = (bf16[48,128,256]{2,1,0:T(8,128)(2,1)S(1)}, bf16[48,128,256]{2,1,0:T(8,128)(2,1)S(1)}) fusion(bf16[48,128,256]{2,1,0:T(8,128)(2,1)} %param.18, pred[48,128]{1,0:T(8,128)(4,1)S(1)} %get-tuple-element.18, bf16[48,256]{1,0:T(8,128)(2,1)S(1)} %bitcast.44, bf16[48,128,256]{2,1,0:T(8,128)(2,1)} %param.17, bf16[48,256]{1,0:T(8,128)(2,1)S(1)} %fusion.70), kind=kLoop, calls=%fused_computation.6 | loop fusion | flops 3145728 | bytes 12638208 | tf_op jit(solution)/shard_map/jit(_where)/select_n | solution.py:71
  31.7 0.0 copy-start.1
  31.7 0.0 copy-start
  31.7 1.6 copy-done.1
  33.4 0.0 copy-done.4
  33.4 1.0 fusion.114
  34.4 0.9 fusion.15
  35.3 1.5 fusion.20
  36.8 0.0 copy-done.5
  36.8 1.8 copy.52
  38.6 1.8 copy.51
  40.4 2.6 pad_maximum_fusion
  43.0 0.0 copy-done
  43.0 0.1 all-gather.3.cloned.1.call-update
  43.1 0.2 all-reduce.2.cloned.1.call-start
  43.3 0.0 copy-done.2
  43.4 10.2 %fusion.35 = f32[48,4096]{1,0:T(8,128)} fusion(bf16[1024,4096]{1,0:T(8,128)(2,1)} %param.16, bf16[4096,1024]{1,0:T(8,128)(2,1)} %param.15, bf16[48,4096]{1,0:T(8,128)(2,1)S(1)} %copy-done.2, f32[4096]{0:T(1024)S(1)} %copy-done.6, f32[4096]{0:T(1024)} %param.11, f32[48]{0:T(128)} %copy-done.8, f32[48]{0:T(128)} %copy-done.7), kind=kOutput, calls=%fused_computation.58 | convolution fusion | flops 809680896 | bytes 17990016 | tf_op jit(solution)/shard_map/dot_general | solution.py:78
  53.5 0.1 all-reduce.2.cloned.1.call-update
  53.6 96.5 %all-gather.3.cloned.1.call-done = f32[768,16,258]{2,1,0:T(8,128)} async-done(((f32[48,16,258]{2,1,0:T(8,128)}), f32[768,16,258]{2,1,0:T(8,128)}) %all-gather.3.cloned.1.call-update) | async-done | bytes 12681232 | tf_op jit(solution)/shard_map/all_gather | solution.py:73
  150.1 12.0 %fusion.111 = (f32[16,48,16,1]{3,2,1,0:T(8,128)}, f32[48,16]{1,0:T(8,128)S(1)}, f32[16,48,16,1]{3,2,1,0:T(8,128)}) fusion(f32[16,48,16,258]{3,2,1,0:T(8,128)} %bitcast.38), kind=kLoop, calls=%fused_computation.146 | loop fusion | flops 11520 | bytes 199680 | tf_op jit(solution)/shard_map/slice | solution.py:52
  162.1 4.9 %copy.63 = f32[16,48,16,1]{1,2,3,0:T(8,128)S(1)} copy(f32[16,48,16,1]{3,2,1,0:T(8,128)} %get-tuple-element.5) | data formatting | bytes 98304
  167.0 0.1 copy.64
  167.1 0.2 copy.54
  167.3 5.9 %fusion = f32[48,16,256]{2,1,0:T(8,128)S(1)} fusion(f32[16,48,16,258]{3,2,1,0:T(8,128)} %bitcast.39, f32[16,48,16]{2,1,0:T(8,128)S(1)} %copy.54), kind=kLoop, calls=%fused_computation.1 | loop fusion | flops 6094848 | bytes 13418496 | tf_op jit(solution)/shard_map/reduce_sum | solution.py:53
  173.2 4.9 %copy.55 = f32[16,48,16,1]{1,2,3,0:T(8,128)S(1)} copy(f32[16,48,16,1]{3,2,1,0:T(8,128)} %get-tuple-element.3) | data formatting | bytes 98304 | tf_op jit(solution)/shard_map/slice | solution.py:52
  178.2 0.1 copy.56
  178.2 0.2 divide_convert_fusion
  178.4 0.1 copy.65
  178.6 77.1 %all-reduce.2.cloned.1.call-done = f32[48,4096]{1,0:T(8,128)} async-done(((f32[48,4096]{1,0:T(8,128)}), f32[48,4096]{1,0:T(8,128)}) %all-reduce.2.cloned.1.call-update) | async-done | bytes 786448 | tf_op jit(solution)/shard_map/psum | solution.py:79
  255.7 14.6 %fusion.2 = bf16[48,4096]{1,0:T(8,128)(2,1)} fusion(f32[48,4096]{1,0:T(8,128)} %all-reduce.2.cloned.1.call-done, bf16[48,4096]{1,0:T(8,128)(2,1)S(1)} %bitcast.40, bf16[4096,4096]{1,0:T(8,128)(2,1)} %param.14, bf16[48,4096]{1,0:T(8,128)(2,1)S(1)} %copy-done.2), kind=kOutput, calls=%fused_computation.5 | convolution fusion | flops 1611399168 | bytes 35520512 | tf_op jit(solution)/shard_map/dot_general | solution.py:75
  (15 shorter events, 0.1 us)
Async XLA Ops:
  7.2 143.0 %all-gather.3.cloned.1.call-start = ((), (), s32[]{:S(2)}) async-start(), calls=%async_computation.1 | async-start | bytes 20054016 | tf_op jit(solution)/shard_map/all_gather | solution.py:73
  9.5 1.3 copy-start.7
  10.8 0.5 copy-start.8
  26.9 0.8 copy-start.3
  27.7 5.6 %copy-start.4 = (bf16[48,18,256]{2,1,0:T(8,128)(2,1)S(1)}, bf16[48,18,256]{2,1,0:T(8,128)(2,1)}, u32[]{:S(2)}) copy-start(bf16[48,18,256]{2,1,0:T(8,128)(2,1)} %copy-done.3) | copy-start | bytes 1327108
  31.7 1.7 copy-start.1
  31.7 11.3 %copy-start = (bf16[48,128,256]{2,1,0:T(8,128)(2,1)}, bf16[48,128,256]{2,1,0:T(8,128)(2,1)S(1)}, u32[]{:S(2)}) copy-start(bf16[48,128,256]{2,1,0:T(8,128)(2,1)S(1)} %get-tuple-element.12) | copy-start | bytes 9437188
  33.4 10.0 %copy-start.2 = (bf16[48,4096]{1,0:T(8,128)(2,1)S(1)}, bf16[48,4096]{1,0:T(8,128)(2,1)}, u32[]{:S(2)}) copy-start(bf16[48,4096]{1,0:T(8,128)(2,1)} %param.10) | copy-start | bytes 1179652
  33.4 10.0 %copy-start.6 = (f32[4096]{0:T(1024)S(1)}, f32[4096]{0:T(1024)}, u32[]{:S(2)}) copy-start(f32[4096]{0:T(1024)} %param.12) | copy-start | bytes 49156
  34.4 2.4 copy-start.5
  43.1 212.6 %all-reduce.2.cloned.1.call-start = ((), (), s32[]{:S(2)}) async-start(), calls=%async_computation | async-start | bytes 1572864 | tf_op jit(solution)/shard_map/psum | solution.py:79
Sparse Core Ops, SparseCore 0:
  43.2 106.8 all-gather.2
  152.5 103.1 all-reduce.1
where the time goes:
time: 278 us; the launch traced here: 277 us
  waiting for transfers between devices  174 us (63%)
  matrix products  42.6 us (15%)
  other arithmetic  29.4 us (11%)
  local copies, waits for them, and re-layouts  16.7 us (6%)
  between operations  14.3 us (5%)
    all_gather x1, waiting for transfers between devices, device_step(): all_stats = lax.all_gather(block_stats, 'sp')  96.5 us
    psum x1, waiting for transfers between devices, device_step(): mlp_out = lax.psum(mlp_part, 'sp')  77.1 us
    dot_general x1, matrix products, device_step(): jnp.dot(normed, w_qkv, preferred_element_type=jnp.float32)  15.4 us
    dot_general x1, matrix products, device_step(): attn_out = jnp.dot(context, w_out, preferred_element_type=jnp.float32)  14.6 us
    slice x1, other arithmetic, combine_stats(): total_sum = jnp.sum(all_stats[..., head_dim + 1] * scale_w, axis=0)  12 us
    dot_general x1, matrix products, device_step(): mlp_part = jnp.dot(activated, w_down, preferred_element_type=jnp.float32)  10.2 us
    unnamed x22, local copies, waits for them, and re-layouts  7.68 us
    reduce_sum x1, other arithmetic, combine_stats(): total_ctx = jnp.sum(all_stats[..., :head_dim] * scale_w[..., None], axis=0)  5.9 us
  transfers between devices with their start and end apart: 2, of which 2 were waited for; matrix products, arithmetic and copies ran while one was open for 14% of the time, Pallas kernels for 0%

commit v1 on v0

v1 whole, which is shorter than its diff:
```python
import functools

import jax
import jax.numpy as jnp
from jax import lax
from jax.experimental import pallas as pl
from jax.experimental.pallas import tpu as pltpu
from jax.sharding import PartitionSpec as P

LN_EPS = 1e-5
ROPE_BASE = 10000.0
NEG_FILL = -1e30
MESH = pl.DeviceIdType.MESH
BLK = 256
HALF = 128
F32 = jnp.float32
BF16 = jnp.bfloat16


def rotary_tables(positions, head_dim):
    inv_freq = 1.0 / (ROPE_BASE ** (jnp.arange(0, head_dim, 2, dtype=F32) / head_dim))
    angles = positions.astype(F32)[:, None] * inv_freq[None, :]
    return jnp.cos(angles), jnp.sin(angles)


def layer_kernel(chips, heads, x_hbm, gamma_hbm, beta_hbm, wqkv_hbm, wout_hbm, wup_hbm, wdown_hbm, k_hbm, v_hbm,
                 cos_ref, sin_ref, lp_ref,
                 out_ref, knew_ref, vnew_ref,
                 x_s, gb_s, h_s, act_s, w_s, k_s, v_s, qk_s, ps_s, pr_s, ss_s, rs_s, ma_s, ost_s, orx_s, cz_s, r_s, g_s, acc_s,
                 in_sem, up_sem, dn_sem, qkv_sem, kv_sem, wo_sem,
                 pd_send, pd_recv, rs_send, rs_recv, ma_send, ma_fsend, ma_recv,
                 qx_send, qx_recv, st_send, st_recv, aa_send, aa_recv, cg_send, cg_fsend, cg_recv):
    rows, d_model = x_hbm.shape
    ff = wup_hbm.shape[1]
    seq = k_hbm.shape[1]
    n_up = ff // BLK
    n_col = d_model // BLK
    half_heads = heads // 2
    slots = (heads + 2) // 2
    tail = rows + 8
    up_rows, dn_rows = d_model, ff
    dn_base = n_up * up_rows
    qkv_base = dn_base + n_col * dn_rows
    n_kv = kv_sem.shape[1]
    kv_rows = rows // n_kv

    s = lax.axis_index('sp')
    z = lax.div(s, 2)
    c = lax.rem(s, 2)
    pc = 1 - c
    partner = {'sp': 2 * z + pc}

    def chip(k):
        return lax.rem(z + k, chips)

    def peer(zz):
        return {'sp': 2 * zz + c}

    def order(i):
        return chip(i + chips // 2)

    def in_copy(i):
        src, dst = ((x_hbm, x_s), (gamma_hbm, gb_s.at[pl.ds(0, 1)]), (beta_hbm, gb_s.at[pl.ds(8, 1)]))[i]
        return pltpu.make_async_copy(src, dst, in_sem.at[i])

    def up_copy(i):
        col = pl.multiple_of(i * BLK, BLK)
        row = pl.multiple_of(i * up_rows, BLK)
        return pltpu.make_async_copy(wup_hbm.at[:, pl.ds(col, BLK)], w_s.at[pl.ds(row, up_rows)], up_sem.at[i])

    def dn_copy(half, i):
        owner = pc if half == 0 else c
        col = pl.multiple_of((owner * chips + order(i)) * BLK, BLK)
        slot = half * chips + i
        row = pl.multiple_of(dn_base + slot * dn_rows, BLK)
        return pltpu.make_async_copy(wdown_hbm.at[:, pl.ds(col, BLK)], w_s.at[pl.ds(row, dn_rows)], dn_sem.at[slot])

    def qkv_copy(i):
        col = pl.multiple_of((c * slots + i) * BLK, BLK)
        row = pl.multiple_of(qkv_base + i * d_model, BLK)
        return pltpu.make_async_copy(wqkv_hbm.at[:, pl.ds(col, BLK)], w_s.at[pl.ds(row, d_model)], qkv_sem.at[i])

    def kv_copy(t, i):
        src, dst = ((k_hbm, k_s), (v_hbm, v_s))[t]
        sl = pl.ds(i * kv_rows, kv_rows)
        return pltpu.make_async_copy(src.at[sl], dst.at[sl], kv_sem.at[t, i])

    def wo_copy(i):
        col = pl.multiple_of(i * BLK, BLK)
        row = pl.multiple_of(i * d_model, BLK)
        return pltpu.make_async_copy(wout_hbm.at[:, pl.ds(col, BLK)], w_s.at[pl.ds(row, d_model)], wo_sem.at[i])

    def pd_copy(zz):
        return pltpu.make_async_remote_copy(ps_s.at[zz], pr_s.at[zz], pd_send.at[zz], pd_recv.at[zz], device_id=partner, device_id_type=MESH)

    def rs_copy(dst, src):
        return pltpu.make_async_remote_copy(ss_s.at[dst], rs_s.at[src], rs_send.at[dst], rs_recv.at[src], device_id=peer(dst), device_id_type=MESH)

    def ma_copy(dst, src):
        slot = c * chips + src
        return pltpu.make_async_remote_copy(ma_s.at[slot], ma_s.at[slot], ma_send.at[dst], ma_recv.at[slot], device_id=peer(dst), device_id_type=MESH)

    def ma_fwd(owner, zz):
        slot = owner * chips + zz
        return pltpu.make_async_remote_copy(ma_s.at[slot], ma_s.at[slot], ma_fsend.at[zz], ma_recv.at[slot], device_id=partner, device_id_type=MESH)

    def qx_copy(owner, i):
        row = pl.multiple_of((owner * slots + i) * 2 * rows, 8)
        ref = qk_s.at[pl.ds(row, 2 * rows)]
        return pltpu.make_async_remote_copy(ref, ref, qx_send.at[i], qx_recv.at[i], device_id=partner, device_id_type=MESH)

    def st_copy():
        return pltpu.make_async_remote_copy(ost_s.at[pc], orx_s, st_send.at[0], st_recv.at[0], device_id=partner, device_id_type=MESH)

    def aa_copy(dst, src):
        a = cz_s.at[pl.ds(pl.multiple_of(dst * 2 * tail, 8), 2 * tail)]
        b = r_s.at[pl.ds(pl.multiple_of(src * 2 * tail, 8), 2 * tail)]
        return pltpu.make_async_remote_copy(a, b, aa_send.at[dst], aa_recv.at[src], device_id=peer(dst), device_id_type=MESH)

    def cg_copy(dst, src):
        slot = c * chips + src
        return pltpu.make_async_remote_copy(g_s.at[slot], g_s.at[slot], cg_send.at[dst], cg_recv.at[slot], device_id=peer(dst), device_id_type=MESH)

    def cg_fwd(owner, zz):
        slot = owner * chips + zz
        return pltpu.make_async_remote_copy(g_s.at[slot], g_s.at[slot], cg_fsend.at[zz], cg_recv.at[slot], device_id=partner, device_id_type=MESH)

    for i in range(3):
        in_copy(i).start()
    bar = pltpu.get_barrier_semaphore()
    pl.semaphore_signal(bar, inc=1, device_id=partner, device_id_type=MESH)
    for k in range(1, chips):
        pl.semaphore_signal(bar, inc=1, device_id=peer(chip(k)), device_id_type=MESH)
    for i in range(n_up):
        up_copy(i).start()
    for half in range(2):
        for i in range(chips):
            dn_copy(half, i).start()
    for i in range(slots):
        qkv_copy(i).start()
    for i in range(n_kv):
        kv_copy(0, i).start()
        kv_copy(1, i).start()
    pl.semaphore_wait(bar, chips)

    for i in range(3):
        in_copy(i).wait()

    @pl.loop(0, rows // 16)
    def _(i):
        sl = pl.ds(pl.multiple_of(i * 16, 16), 16)
        xf = x_s[sl, :].astype(F32)
        mean = jnp.mean(xf, axis=-1, keepdims=True)
        cen = xf - mean
        var = jnp.mean(cen * cen, axis=-1, keepdims=True)
        h_s[sl, :] = (cen * lax.rsqrt(var + LN_EPS) * gb_s[0:1, :] + gb_s[8:9, :]).astype(BF16)

    def chunk_dot(a_ref, row, depth):
        acc = None
        for kk in range(depth // BLK):
            w = w_s[pl.ds(pl.multiple_of(row + kk * BLK, BLK), BLK), :]
            p = jnp.dot(a_ref[:, kk * BLK:(kk + 1) * BLK], w, preferred_element_type=F32)
            acc = p if acc is None else acc + p
        return acc

    @pl.loop(0, n_up)
    def _(i):
        up_copy(i).wait()
        u = chunk_dot(h_s, i * up_rows, up_rows)
        g = 0.5 * u * (1.0 + lax.erf(u * (0.5 ** 0.5)))
        act_s[:, pl.ds(pl.multiple_of(i * BLK, BLK), BLK)] = g.astype(BF16)

    @pl.loop(0, chips)
    def _(i):
        dn_copy(0, i).wait()
        zz = order(i)
        ps_s[zz] = chunk_dot(act_s, dn_base + i * dn_rows, dn_rows)
        pd_copy(zz).start()

    @pl.loop(0, chips)
    def _(i):
        dn_copy(1, i).wait()
        zz = order(i)
        p = chunk_dot(act_s, dn_base + (chips + i) * dn_rows, dn_rows)
        pd_copy(zz).wait_recv()
        p = p + pr_s[zz]

        @pl.when(zz == z)
        def _():
            rs_s[z] = p

        @pl.when(zz != z)
        def _():
            ss_s[zz] = p
            rs_copy(zz, z).start()

    @pl.loop(0, slots)
    def _(i):
        qkv_copy(i).wait()
        a = chunk_dot(h_s, qkv_base + i * d_model, d_model).astype(BF16).astype(F32)
        a1, a2 = a[:, :HALF], a[:, HALF:]
        cs, sn = cos_ref[...], sin_ref[...]
        r1 = (a1 * cs - a2 * sn).astype(BF16).astype(F32)
        r2 = (a2 * cs + a1 * sn).astype(BF16).astype(F32)
        slot = c * slots + i
        is_v = slot == heads + 1
        row = pl.multiple_of(slot * 2 * rows, 8)
        qk_s[pl.ds(row, rows), :] = jnp.where(is_v, a1, r1)
        qk_s[pl.ds(row + rows, rows), :] = jnp.where(is_v, a2, r2)
        qx_copy(c, i).start()

    for i in range(n_col):
        wo_copy(i).start()

    for i in range(slots):
        qx_copy(pc, i).wait_recv()
    for t in range(2):
        sl = slice(t * HALF, (t + 1) * HALF)
        knew_ref[:, sl] = qk_s[(2 * heads + t) * rows:(2 * heads + t + 1) * rows, :].astype(BF16)
        vnew_ref[:, sl] = qk_s[(2 * heads + 2 + t) * rows:(2 * heads + 3 + t) * rows, :].astype(BF16)

    lane = lax.broadcasted_iota(jnp.int32, (heads, seq), 1)
    scale = k_s.shape[2] ** -0.5

    def attend(b, carry):
        mm, ll = carry
        def both(base, n):
            return jnp.concatenate([qk_s[pl.ds(base + b, n, stride=2 * rows), :], qk_s[pl.ds(base + rows + b, n, stride=2 * rows), :]], axis=-1)

        def one(base):
            return jnp.concatenate([qk_s[pl.ds(base + b, 1), :], qk_s[pl.ds(base + rows + b, 1), :]], axis=-1)

        q = both(0, heads)
        kn = one(2 * heads * rows)
        vn = one((2 * heads + 2) * rows)
        lp = lp_ref[pl.ds(b, 1), :]
        sc = lax.dot_general(q.astype(BF16), k_s[b], (((1,), (1,)), ((), ())), preferred_element_type=F32)
        here = lane == lp
        sc = jnp.where(here, jnp.sum(q * kn, axis=-1, keepdims=True), sc) * scale
        valid = lane <= lp
        sc = jnp.where(valid, sc, NEG_FILL)
        m = jnp.max(sc, axis=-1, keepdims=True)
        e = jnp.where(valid, jnp.exp(sc - m), 0.0)
        l = jnp.sum(e, axis=-1, keepdims=True)
        eb = e.astype(BF16).astype(F32)
        e_new = jnp.sum(jnp.where(here, eb, 0.0), axis=-1, keepdims=True)
        o = jnp.dot(jnp.where(here, 0.0, eb).astype(BF16), v_s[b], preferred_element_type=F32) + e_new * vn
        ost_s[0, pl.ds(pl.multiple_of(b * half_heads, 8), half_heads), :] = o[:half_heads]
        ost_s[1, pl.ds(pl.multiple_of(b * half_heads, 8), half_heads), :] = o[half_heads:]
        col = lane == b
        return jnp.where(col, m, mm), jnp.where(col, l, ll)

    zero = jnp.zeros((heads, seq), F32)
    carry = (zero, zero)
    for i in range(n_kv):
        kv_copy(0, i).wait()
        kv_copy(1, i).wait()
        carry = lax.fori_loop(i * kv_rows, (i + 1) * kv_rows, attend, carry, unroll=4)
    mm, ll = carry
    ml = jnp.concatenate([mm, ll], axis=-1)
    ost_s[0, rows * half_heads:, :] = ml[:half_heads]
    ost_s[1, rows * half_heads:, :] = ml[half_heads:]
    st_copy().start()

    for k in range(1, chips):
        rs_copy(chip(k), chip(k)).wait_recv()
    tot = rs_s[0]
    for j in range(1, chips):
        tot = tot + rs_s[j]
    ma_s[c * chips + z] = tot
    for k in range(1, chips):
        ma_copy(chip(k), z).start()
    ma_fwd(c, z).start()

    st_copy().wait_recv()
    base = rows * half_heads
    m_s, l_s = ost_s[c, base:, :HALF], ost_s[c, base:, HALF:]
    m_p, l_p = orx_s[base:, :HALF], orx_s[base:, HALF:]
    m_c = jnp.maximum(m_s, m_p)
    w_own, w_par = jnp.exp(m_s - m_c), jnp.exp(m_p - m_c)
    def put(b, lo, hi):
        cz_s[pl.ds(b, half_heads, stride=2 * tail), :] = lo
        cz_s[pl.ds(tail + b, half_heads, stride=2 * tail), :] = hi

    for b in range(rows):
        sl = slice(b * half_heads, (b + 1) * half_heads)
        mix = ost_s[c, sl, :] * w_own[:, b:b + 1] + orx_s[sl, :] * w_par[:, b:b + 1]
        put(b, mix[:, :HALF], mix[:, HALF:])
    put(rows, m_c, l_s * w_own + l_p * w_par)
    nil = jnp.zeros((half_heads, HALF), F32)
    for b in range(rows + 1, tail):
        put(b, nil, nil)
    for k in range(1, chips):
        aa_copy(chip(k), z).start()
    mine = pl.ds(pl.multiple_of(z * 2 * tail, 8), 2 * tail)
    r_s[mine, :] = cz_s[mine, :]

    for k in range(1, chips):
        aa_copy(chip(k), chip(k)).wait_recv()
    m_all = r_s[pl.ds(rows, chips, stride=2 * tail), :]
    l_all = r_s[pl.ds(tail + rows, chips, stride=2 * tail), :]
    w_all = jnp.exp(m_all - jnp.max(m_all, axis=0, keepdims=True))
    l_tot = jnp.sum(l_all * w_all, axis=0, keepdims=True)
    w_t = jnp.transpose(w_all)[:rows]
    l_t = jnp.transpose(jnp.broadcast_to(l_tot, w_all.shape))[:rows]
    for t in range(2):
        ctx = None
        for j in range(chips):
            at = (2 * j + t) * tail
            part = r_s[at:at + rows, :] * w_t[:, j:j + 1]
            ctx = part if ctx is None else ctx + part
        g_s[c * chips + z, :, t * HALF:(t + 1) * HALF] = (ctx / l_t[:, 0:1]).astype(BF16).astype(F32)
    for k in range(1, chips):
        cg_copy(chip(k), z).start()
    cg_fwd(c, z).start()

    for i in range(n_col):
        wo_copy(i).wait()

    def out_dot(slot, first=False):
        a = g_s[slot].astype(BF16)
        for n in range(n_col):
            w = w_s[pl.ds(pl.multiple_of(n * d_model + slot * BLK, BLK), BLK), :]
            p = jnp.dot(a, w, preferred_element_type=F32)
            sl = slice(n * BLK, (n + 1) * BLK)
            acc_s[:, sl] = p if first else acc_s[:, sl] + p

    out_dot(c * chips + z, True)
    for k in range(1, chips):
        ma_copy(chip(k), chip(k)).wait_recv()
        ma_fwd(c, chip(k)).start()

    @pl.loop(1, chips)
    def _(k):
        cg_copy(chip(k), chip(k)).wait_recv()
        cg_fwd(c, chip(k)).start()
        out_dot(c * chips + chip(k))

    @pl.loop(0, chips)
    def _(k):
        cg_fwd(pc, chip(k)).wait_recv()
        out_dot(pc * chips + chip(k))

    for k in range(chips):
        ma_fwd(pc, chip(k)).wait_recv()
    for n in range(n_col):
        sl = slice(n * BLK, (n + 1) * BLK)
        out_ref[:, sl] = (x_s[:, sl].astype(F32) + acc_s[:, sl] + ma_s[n]).astype(BF16)

    for k in range(chips):
        pd_copy(chip(k)).wait_send()
        ma_fwd(c, chip(k)).wait_send()
        cg_fwd(c, chip(k)).wait_send()
    for k in range(1, chips):
        rs_copy(chip(k), z).wait_send()
        ma_copy(chip(k), z).wait_send()
        aa_copy(chip(k), z).wait_send()
        cg_copy(chip(k), z).wait_send()
    for i in range(slots):
        qx_copy(c, i).wait_send()
    st_copy().wait_send()


def device_step(n_sp, hidden, ln_gamma, ln_beta, w_qkv, w_out, w_up, w_down, k_cache, v_cache, positions):
    rows, d_model = hidden.shape
    seq, head_dim = k_cache.shape[1], k_cache.shape[2]
    heads = w_out.shape[0] // head_dim
    ff = w_up.shape[1]
    chips = n_sp // 2
    slots = (heads + 2) // 2
    assert head_dim == BLK and heads == n_sp and d_model == n_sp * BLK
    cos, sin = rotary_tables(positions, head_dim)
    local_pos = positions - lax.axis_index('sp') * seq
    lp = jnp.broadcast_to(local_pos[:, None], (rows, seq))
    n_up, n_col = ff // BLK, d_model // BLK
    w_rows = n_up * d_model + n_col * ff + slots * d_model
    n_kv = 3
    half = heads // 2
    any_spec = pl.BlockSpec(memory_space=pl.ANY)
    vmem_spec = pl.BlockSpec(memory_space=pltpu.VMEM)
    dma = pltpu.SemaphoreType.DMA
    scratch = [
        pltpu.VMEM((rows, d_model), BF16),
        pltpu.VMEM((16, d_model), F32),
        pltpu.VMEM((rows, d_model), BF16),
        pltpu.VMEM((rows, ff), BF16),
        pltpu.VMEM((w_rows, BLK), BF16),
        pltpu.VMEM(k_cache.shape, BF16),
        pltpu.VMEM(v_cache.shape, BF16),
        pltpu.VMEM(((heads + 2) * 2 * rows, HALF), F32),
        pltpu.VMEM((chips, rows, BLK), F32),
        pltpu.VMEM((chips, rows, BLK), F32),
        pltpu.VMEM((chips, rows, BLK), F32),
        pltpu.VMEM((chips, rows, BLK), F32),
        pltpu.VMEM((n_sp, rows, BLK), F32),
        pltpu.VMEM((2, (rows + 1) * half, BLK), F32),
        pltpu.VMEM(((rows + 1) * half, BLK), F32),
        pltpu.VMEM((chips * 2 * (rows + 8), HALF), F32),
        pltpu.VMEM((chips * 2 * (rows + 8), HALF), F32),
        pltpu.VMEM((n_sp, rows, BLK), F32),
        pltpu.VMEM((rows, d_model), F32),
        dma((3,)), dma((n_up,)), dma((n_col,)), dma((slots,)), dma((2, n_kv)), dma((n_col,)),
        dma((chips,)), dma((chips,)), dma((chips,)), dma((chips,)), dma((chips,)), dma((chips,)), dma((n_sp,)),
        dma((slots,)), dma((slots,)), dma((1,)), dma((1,)), dma((chips,)), dma((chips,)), dma((chips,)), dma((chips,)), dma((n_sp,)),
    ]
    out, k_new, v_new = pl.pallas_call(
        functools.partial(layer_kernel, chips, heads),
        out_shape=(jax.ShapeDtypeStruct((rows, d_model), BF16), jax.ShapeDtypeStruct((rows, BLK), BF16), jax.ShapeDtypeStruct((rows, BLK), BF16)),
        in_specs=[any_spec] * 9 + [vmem_spec] * 3,
        out_specs=(vmem_spec, vmem_spec, vmem_spec),
        scratch_shapes=scratch,
        compiler_params=pltpu.CompilerParams(collective_id=0, has_side_effects=True, vmem_limit_bytes=63 * 1024 * 1024),
        name='decode_layer',
    )(hidden, ln_gamma.reshape(1, -1), ln_beta.reshape(1, -1), w_qkv, w_out, w_up, w_down, k_cache, v_cache, cos, sin, lp)
    write_mask = (jnp.arange(seq)[None, :] == local_pos[:, None])[:, :, None]
    k_next = jnp.where(write_mask, k_new[:, None, :], k_cache)
    v_next = jnp.where(write_mask, v_new[:, None, :], v_cache)
    return out, k_next, v_next


def solution(mesh):
    cache_spec = P('dp', 'sp', None)
    in_specs = (P('dp', None), P(None), P(None), P(None, None), P(None, None), P(None, 'sp'), P('sp', None), cache_spec, cache_spec, P('dp'))
    out_specs = (P('dp', None), cache_spec, cache_spec)
    return jax.shard_map(functools.partial(device_step, mesh.shape['sp']), mesh=mesh, in_specs=in_specs, out_specs=out_specs, check_vma=False)
```

time: 278 us -> 86.2 us (0.31)
  waiting for transfers between devices: 174 us -> 0 us
  Pallas kernels: 0 us -> 75.5 us
  matrix products: 42.6 us -> 0 us
  other arithmetic: 29.4 us -> 8.39 us
  local copies, waits for them, and re-layouts: 16.7 us -> 1.43 us
  between operations: 14.3 us -> 0.66 us
    all_gather x1 -> x0, waiting for transfers between devices: 96.5 us -> none  [device_step(): all_stats = lax.all_gather(block_stats, 'sp')]
    psum x1 -> x0, waiting for transfers between devices: 77.1 us -> none  [device_step(): mlp_out = lax.psum(mlp_part, 'sp')]
    pallas_call x0 -> x1, Pallas kernels: none -> 75.5 us  [device_step(): pl.pallas_call(functools.partial(layer_kernel, chips, heads), out_shape=(...]
    dot_general x5 -> x0, matrix products: 42.6 us -> none  [the longest x1 15.4 us: device_step(): jnp.dot(normed, w_qkv, preferred_element_type=jnp.float32)]
    slice x2 -> x0, other arithmetic: 12 us -> none  [the longest x1 12 us: combine_stats(): total_sum = jnp.sum(all_stats[..., head_dim + 1] * scale_w, axis=0)]
    reduce_sum x5 -> x0, other arithmetic: 9.28 us -> none  [the longest x1 5.9 us: combine_stats(): total_ctx = jnp.sum(all_stats[..., :head_dim] * scale_w[..., None], axis=0)]
    unnamed x22 -> x3, local copies, waits for them, and re-layouts: 7.68 us -> 0.75 us
    slice x1 -> x0, local copies, waits for them, and re-layouts: 4.9 us -> none  [combine_stats(): total_sum = jnp.sum(all_stats[..., head_dim + 1] * scale_w, axis=0)]
  transfers between devices with their start and end apart: 2 -> 0, of which waited for: 2 -> 0; matrix products, arithmetic and copies ran while one was open for 14% -> 0% of each run, Pallas kernels for 0% -> 0%
where the time goes in v1:
time: 86.2 us; the launch traced here: 86 us
  Pallas kernels  75.5 us (88%)
  other arithmetic  8.39 us (10%)
  local copies, waits for them, and re-layouts  1.43 us (2%)
    pallas_call x1, Pallas kernels, device_step(): pl.pallas_call(functools.partial(layer_kernel, chips, heads), out_shape=(...  75.5 us
    select_n x1, other arithmetic, device_step(): v_next = jnp.where(write_mask, v_new[:, None, :], v_cache)  6.78 us

profile of v1, /device:TPU:21, one launch (start us, length us, event | category | flops | bytes accessed | tf_op | source)
XLA Modules:
  0.0 86.0 jit_solution(933347858435552542)
XLA Ops:
  0.6 0.7 broadcast_subtract_fusion
  1.4 0.1 iota_compare_fusion
  1.5 0.7 broadcast_in_dim.37.lp_ref
  2.1 0.8 multiply_sine_fusion
  2.9 75.5 %decode_layer.1 = (bf16[48,4096]{1,0:T(8,128)(2,1)}, bf16[48,256]{1,0:T(8,128)(2,1)}, bf16[48,256]{1,0:T(8,128)(2,1)}) custom-call(bf16[48,4096]{1,0:T(8,128)(2,1)} %x_hbm.1, f32[1,4096]{1,0:T(1,128)} %bitcast.2, f32[1,4096]{1,0:T(1,128)} %bitcast.3, bf16[4096,4608]{1,0:T(8,128)(2,1)} %wqkv_hbm.1, bf16[4096,4096]{1,0:T(8,128)(2,1)} %wout_hbm.1, ...), custom_call_target="tpu_custom_call" | custom-call | tf_op jit(solution)/shard_map/decode_layer/pallas_call | solution.py:406
  78.5 0.0 copy-start
  78.5 6.8 %broadcast_select_fusion = (bf16[48,128,256]{2,1,0:T(8,128)(2,1)}, bf16[48,128,256]{2,1,0:T(8,128)(2,1)}) fusion(bf16[48,128,256]{2,1,0:T(8,128)(2,1)} %v_hbm.1, pred[48,128]{1,0:T(8,128)(4,1)S(1)} %iota_compare_fusion, bf16[48,256]{1,0:T(8,128)(2,1)} %get-tuple-element.8, bf16[48,128,256]{2,1,0:T(8,128)(2,1)} %k_hbm.1, bf16[48,256]{1,0:T(8,128)(2,1)} %get-tuple-element.7), kind=kLoop, calls=%fused_computation | loop fusion | flops 3145728 | bytes 12638208 | tf_op jit(solution)/shard_map/jit(_where)/select_n | solution.py:417
  85.2 0.0 copy-done
  85.2 0.7 copy.14
  (1 shorter events, 0.0 us)
Async XLA Ops:
  78.5 6.8 %copy-start = (bf16[48,4096]{1,0:T(8,128)(2,1)S(1)}, bf16[48,4096]{1,0:T(8,128)(2,1)}, u32[]{:S(2)}) copy-start(bf16[48,4096]{1,0:T(8,128)(2,1)} %get-tuple-element.18) | copy-start | bytes 1179652

commit v2 on v1

v2 whole, which is shorter than its diff:
```python
import functools

import jax
import jax.numpy as jnp
from jax import lax
from jax.experimental import pallas as pl
from jax.experimental.pallas import tpu as pltpu
from jax.sharding import PartitionSpec as P

LN_EPS = 1e-5
ROPE_BASE = 10000.0
NEG_FILL = -1e30
MESH = pl.DeviceIdType.MESH
BLK = 256
HALF = 128
F32 = jnp.float32
BF16 = jnp.bfloat16


ORDER = (3, -3, 4, 2, -2, 1, -1, 0)


class Phases:
    def __init__(self):
        self.scope = None

    def __call__(self, name):
        if self.scope is not None:
            self.scope.__exit__(None, None, None)
        self.scope = jax.named_scope(name) if name else None
        if self.scope is not None:
            self.scope.__enter__()


def layer_kernel(chips, heads, x_hbm, gamma_hbm, beta_hbm, wqkv_hbm, wout_hbm, wup_hbm, wdown_hbm, k_hbm, v_hbm, pos_hbm,
                 inv_ref, out_ref, knew_ref, vnew_ref,
                 x_s, gb_s, h_s, act_s, w_s, k_s, v_s, pos_s, lp_s, cs_s, sn_s, qk_s,
                 ps_s, pr_s, ss_s, ra_s, rb_s, ma_s, ost_s, orx_s, cz_s, ta_s, tb_s, tw_s, g_s, acc_s,
                 in_sem, up_sem, dn_sem, qkv_sem, kv_sem, wo_sem,
                 pd_send, pd_recv, qx_send, qx_recv, st_send, st_recv,
                 rs_send, rs_recv, aa_send, aa_recv, ma_send, ma_recv, mf_send, mf_recv, cg_send, cg_recv, cf_send, cf_recv):
    rows, d_model = x_hbm.shape
    ff = wup_hbm.shape[1]
    seq = k_hbm.shape[1]
    n_up = ff // BLK
    n_col = d_model // BLK
    half_heads = heads // 2
    slots = (heads + 2) // 2
    hr = rows // 2
    ml_at = 2 * hr
    hi_at = ml_at + 8
    chunk = 4 * hr + 8
    part = 2 * hr + 8
    up_rows, dn_rows = d_model, ff
    dn_base = n_up * up_rows
    qkv_base = dn_base + n_col * dn_rows
    n_kv = kv_sem.shape[1]
    kv_rows = rows // n_kv

    s = lax.axis_index('sp')
    z = lax.div(s, 2)
    c = lax.rem(s, 2)
    pc = 1 - c
    partner = {'sp': 2 * z + pc}

    def chip(k):
        return lax.rem(z + (k % chips), chips)

    def peer(k):
        return {'sp': 2 * chip(k) + c}

    def in_copy(i):
        src, dst = ((x_hbm, x_s), (gamma_hbm, gb_s.at[pl.ds(0, 1)]), (beta_hbm, gb_s.at[pl.ds(8, 1)]), (pos_hbm, pos_s))[i]
        return pltpu.make_async_copy(src, dst, in_sem.at[i])

    def up_copy(i):
        col = pl.multiple_of(i * BLK, BLK)
        row = pl.multiple_of(i * up_rows, BLK)
        return pltpu.make_async_copy(wup_hbm.at[:, pl.ds(col, BLK)], w_s.at[pl.ds(row, up_rows)], up_sem.at[i])

    def dn_copy(half, i):
        owner = pc if half == 0 else c
        col = pl.multiple_of((owner * chips + chip(ORDER[i])) * BLK, BLK)
        slot = half * chips + i
        row = pl.multiple_of(dn_base + slot * dn_rows, BLK)
        return pltpu.make_async_copy(wdown_hbm.at[:, pl.ds(col, BLK)], w_s.at[pl.ds(row, dn_rows)], dn_sem.at[slot])

    def qkv_copy(i):
        col = pl.multiple_of((c * slots + i) * BLK, BLK)
        row = pl.multiple_of(qkv_base + i * d_model, BLK)
        return pltpu.make_async_copy(wqkv_hbm.at[:, pl.ds(col, BLK)], w_s.at[pl.ds(row, d_model)], qkv_sem.at[i])

    def kv_copy(t, i):
        src, dst = ((k_hbm, k_s), (v_hbm, v_s))[t]
        sl = pl.ds(i * kv_rows, kv_rows)
        return pltpu.make_async_copy(src.at[sl], dst.at[sl], kv_sem.at[t, i])

    def wo_copy(i):
        col = pl.multiple_of(i * BLK, BLK)
        row = pl.multiple_of(i * d_model, BLK)
        return pltpu.make_async_copy(wout_hbm.at[:, pl.ds(col, BLK)], w_s.at[pl.ds(row, d_model)], wo_sem.at[i])

    def remote(src, dst, send, recv, to):
        return pltpu.make_async_remote_copy(src, dst, send, recv, device_id=to, device_id_type=MESH)

    def pd_copy(i):
        return remote(ps_s.at[i], pr_s.at[i], pd_send.at[i], pd_recv.at[i], partner)

    def qx_copy(owner, i):
        row = pl.multiple_of((owner * slots + i) * 2 * rows, 8)
        ref = qk_s.at[pl.ds(row, 2 * rows)]
        return remote(ref, ref, qx_send.at[i], qx_recv.at[i], partner)

    def st_copy():
        return remote(ost_s.at[pc], orx_s, st_send.at[0], st_recv.at[0], partner)

    hops = (1, -1, 2, -2, 2, -2, 1, -1)

    def rs_copy(i):
        src = (ss_s.at[0], ss_s.at[1], ss_s.at[2, pl.ds(0, hr)], ss_s.at[2, pl.ds(hr, hr)], ss_s.at[3], ss_s.at[4], ss_s.at[5], ss_s.at[6])[i]
        dst = (ra_s.at[0], ra_s.at[1], ra_s.at[2, pl.ds(0, hr)], ra_s.at[2, pl.ds(hr, hr)], rb_s.at[0], rb_s.at[1], rb_s.at[2], rb_s.at[3])[i]
        return remote(src, dst, rs_send.at[i], rs_recv.at[i], peer(hops[i]))

    def cz_at(k, off, n):
        return cz_s.at[pl.ds(pl.multiple_of(chip(k) * chunk + off, 8), n)]

    def aa_copy(i):
        src = (lambda: cz_at(3, 0, chunk), lambda: cz_at(-3, 0, chunk), lambda: cz_at(4, 0, part), lambda: cz_at(4, ml_at, part),
               lambda: tw_s.at[0], lambda: tw_s.at[1], lambda: cz_at(1, 0, chunk), lambda: cz_at(-1, 0, chunk))[i]()
        dst = (ta_s.at[0], ta_s.at[1], ta_s.at[2, pl.ds(0, part)], ta_s.at[3, pl.ds(0, part)], tb_s.at[0], tb_s.at[1], tb_s.at[2], tb_s.at[3])[i]
        return remote(src, dst, aa_send.at[i], aa_recv.at[i], peer(hops[i]))

    g_hop = (2, -2, 1, -1, 1, -1, 2, -2)
    g_src = (0, 0, 0, 0, -2, 2, -2, 2)

    def gather_copy(buf, send, recv, i):
        ref = buf.at[c * chips + chip(g_src[i])]
        if i >= 6:
            ref = ref.at[pl.ds((i - 6) * hr, hr)]
        return remote(ref, ref, send.at[i], recv.at[i], peer(g_hop[i]))

    def gather_recv(buf, send, recv, i):
        ref = buf.at[c * chips + chip(g_src[i] - g_hop[i])]
        if i >= 6:
            ref = ref.at[pl.ds((i - 6) * hr, hr)]
        return remote(ref, ref, send.at[i], recv.at[i], peer(g_hop[i]))

    def ma_copy(i):
        return gather_copy(ma_s, ma_send, ma_recv, i)

    def cg_copy(i):
        return gather_copy(g_s, cg_send, cg_recv, i)

    def ma_wait(i):
        gather_recv(ma_s, ma_send, ma_recv, i).wait_recv()

    def cg_wait(i):
        gather_recv(g_s, cg_send, cg_recv, i).wait_recv()

    def ma_fwd(owner, k):
        ref = ma_s.at[owner * chips + chip(k)]
        return remote(ref, ref, mf_send.at[k % chips], mf_recv.at[k % chips], partner)

    def cg_fwd(owner, k):
        ref = g_s.at[owner * chips + chip(k)]
        return remote(ref, ref, cf_send.at[k % chips], cf_recv.at[k % chips], partner)

    ph = Phases()
    ph('entry')
    for i in range(4):
        in_copy(i).start()
    for i in range(n_up):
        up_copy(i).start()
    bar = pltpu.get_barrier_semaphore()
    pl.semaphore_signal(bar, inc=1, device_id=partner, device_id_type=MESH)
    for k in (1, -1, 2, -2):
        pl.semaphore_signal(bar, inc=1, device_id=peer(k), device_id_type=MESH)
    for half in range(2):
        for i in range(chips):
            dn_copy(half, i).start()
    for i in range(slots):
        qkv_copy(i).start()
    for i in range(n_kv):
        kv_copy(0, i).start()
        kv_copy(1, i).start()

    ph('in_wait')
    for i in range(4):
        in_copy(i).wait()
    ph('layer_norm')

    @pl.loop(0, rows // 16)
    def _(i):
        sl = pl.ds(pl.multiple_of(i * 16, 16), 16)
        xf = x_s[sl, :].astype(F32)
        mean = jnp.mean(xf, axis=-1, keepdims=True)
        cen = xf - mean
        var = jnp.mean(cen * cen, axis=-1, keepdims=True)
        h_s[sl, :] = (cen * lax.rsqrt(var + LN_EPS) * gb_s[0:1, :] + gb_s[8:9, :]).astype(BF16)

    ph('rope')
    for b in range(rows):
        lp_s[b:b + 1, :] = jnp.full((1, HALF), pos_s[b], jnp.int32).astype(F32)
    ang = lp_s[...] * inv_ref[...]
    cs_s[...] = jnp.cos(ang)
    sn_s[...] = jnp.sin(ang)
    lp_s[...] = lp_s[...] - (s * seq).astype(F32)

    def chunk_dots(a_ref, bases, depth):
        accs = [None] * len(bases)
        for kk in range(depth // BLK):
            a = a_ref[:, kk * BLK:(kk + 1) * BLK]
            for j, row in enumerate(bases):
                w = w_s[pl.ds(pl.multiple_of(row + kk * BLK, BLK), BLK), :]
                p = jnp.dot(a, w, preferred_element_type=F32)
                accs[j] = p if accs[j] is None else accs[j] + p
        return accs

    ph('mlp_up')

    @pl.loop(0, n_up // 2)
    def _(i):
        up_copy(2 * i).wait()
        up_copy(2 * i + 1).wait()
        us = chunk_dots(h_s, [(2 * i + j) * up_rows for j in range(2)], up_rows)
        for j, u in enumerate(us):
            g = 0.5 * u * (1.0 + lax.erf(u * (0.5 ** 0.5)))
            act_s[:, pl.ds(pl.multiple_of((2 * i + j) * BLK, BLK), BLK)] = g.astype(BF16)

    ph('barrier')
    pl.semaphore_wait(bar, 5)
    ph('down_partner')
    for i in range(0, chips, 2):
        for j in range(2):
            dn_copy(0, i + j).wait()
        for j, p in enumerate(chunk_dots(act_s, [dn_base + (i + j) * dn_rows for j in range(2)], dn_rows)):
            ps_s[i + j] = p
            pd_copy(i + j).start()

    ph('down_own')
    for i in range(0, chips, 2):
        for j in range(2):
            dn_copy(1, i + j).wait()
        for j, p in enumerate(chunk_dots(act_s, [dn_base + (chips + i + j) * dn_rows for j in range(2)], dn_rows)):
            n = i + j
            pd_copy(n).wait_recv()
            ss_s[n] = p + pr_s[n]
            for m in ((0,), (1,), (2, 3), (), (), (6,), (7,), ())[n]:
                rs_copy(m).start()

    def qkv_store(i, acc):
        a = acc.astype(BF16).astype(F32)
        a1, a2 = a[:, :HALF], a[:, HALF:]
        cs, sn = cs_s[...], sn_s[...]
        r1 = (a1 * cs - a2 * sn).astype(BF16).astype(F32)
        r2 = (a2 * cs + a1 * sn).astype(BF16).astype(F32)
        slot = c * slots + i
        is_v = slot == heads + 1
        row = pl.multiple_of(slot * 2 * rows, 8)
        qk_s[pl.ds(row, rows), :] = jnp.where(is_v, a1, r1)
        qk_s[pl.ds(row + rows, rows), :] = jnp.where(is_v, a2, r2)
        qx_copy(c, i).start()

    def qkv_pair(i):
        qkv_copy(2 * i).wait()
        qkv_copy(2 * i + 1).wait()
        for j, acc in enumerate(chunk_dots(h_s, [qkv_base + (2 * i + j) * d_model for j in range(2)], d_model)):
            qkv_store(2 * i + j, acc)

    n_pair = slots // 2
    ph('qkv')
    pl.loop(0, n_pair - 1)(qkv_pair)

    ph('rs_add')
    for i in range(4):
        rs_copy(i).wait_recv()
    ss_s[3, 0:hr] = ss_s[3, 0:hr] + ra_s[0, 0:hr] + ra_s[2, 0:hr]
    ss_s[3, hr:] = ss_s[3, hr:] + ra_s[0, hr:]
    ss_s[4, 0:hr] = ss_s[4, 0:hr] + ra_s[1, 0:hr]
    ss_s[4, hr:] = ss_s[4, hr:] + ra_s[1, hr:] + ra_s[2, hr:]
    rs_copy(4).start()
    rs_copy(5).start()
    ph('qkv_last')
    qkv_pair(n_pair - 1)
    for i in range(2 * n_pair, slots):
        qkv_copy(i).wait()
        qkv_store(i, chunk_dots(h_s, [qkv_base + i * d_model], d_model)[0])

    for i in range(n_col):
        wo_copy(i).start()

    ph('qkv_wait')
    for i in range(slots):
        qx_copy(pc, i).wait_recv()
    for t in range(2):
        sl = slice(t * HALF, (t + 1) * HALF)
        knew_ref[:, sl] = qk_s[(2 * heads + t) * rows:(2 * heads + t + 1) * rows, :].astype(BF16)
        vnew_ref[:, sl] = qk_s[(2 * heads + 2 + t) * rows:(2 * heads + 3 + t) * rows, :].astype(BF16)

    lane = lax.broadcasted_iota(jnp.int32, (heads, seq), 1)
    lane_f = lane.astype(F32)
    scale = k_s.shape[2] ** -0.5
    group = rows // 4

    def attend(g, carry):
        mm, ll = carry
        base = g * group
        scores, values, here = [], [], []
        for r in range(group):
            b = base + r

            def both(at, n):
                return jnp.concatenate([qk_s[pl.ds(at + b, n, stride=2 * rows), :], qk_s[pl.ds(at + rows + b, n, stride=2 * rows), :]], axis=-1)

            def one(at):
                return jnp.concatenate([qk_s[pl.ds(at + b, 1), :], qk_s[pl.ds(at + rows + b, 1), :]], axis=-1)

            q = both(0, heads)
            kn = one(2 * heads * rows)
            lp = lp_s[pl.ds(b, 1), :]
            here.append(lane_f == lp)
            sc = lax.dot_general(q.astype(BF16), k_s[b], (((1,), (1,)), ((), ())), preferred_element_type=F32)
            sc = jnp.where(here[r], jnp.sum(q * kn, axis=-1, keepdims=True), sc) * scale
            scores.append(jnp.where(lane_f <= lp, sc, NEG_FILL))
            values.append(one((2 * heads + 2) * rows))
        es, news = [], []
        for r in range(group):
            m = jnp.max(scores[r], axis=-1, keepdims=True)
            e = jnp.where(lane_f <= lp_s[pl.ds(base + r, 1), :], jnp.exp(scores[r] - m), 0.0)
            col = lane == base + r
            mm = jnp.where(col, m, mm)
            ll = jnp.where(col, jnp.sum(e, axis=-1, keepdims=True), ll)
            eb = e.astype(BF16).astype(F32)
            news.append(jnp.sum(jnp.where(here[r], eb, 0.0), axis=-1, keepdims=True))
            es.append(jnp.where(here[r], 0.0, eb).astype(BF16))
        for r in range(group):
            b = base + r
            o = jnp.dot(es[r], v_s[b], preferred_element_type=F32) + news[r] * values[r]
            at = pl.ds(pl.multiple_of(b * half_heads, 8), half_heads)
            ost_s[0, at, :] = o[:half_heads]
            ost_s[1, at, :] = o[half_heads:]
        return mm, ll

    ph('kv_wait')
    for i in range(n_kv):
        kv_copy(0, i).wait()
        kv_copy(1, i).wait()
    ph('attention')
    zero = jnp.zeros((heads, seq), F32)
    mm, ll = lax.fori_loop(0, 3, attend, (zero, zero))

    ph('rs_sum')
    for i in range(4, 8):
        rs_copy(i).wait_recv()
    ma_s[c * chips + z] = ss_s[7] + rb_s[0] + rb_s[1] + rb_s[2] + rb_s[3]
    for i in range(4):
        ma_copy(i).start()
    ma_fwd(c, 0).start()

    ph('attention_last')
    mm, ll = lax.fori_loop(3, 4, attend, (mm, ll))
    ml = jnp.concatenate([mm, ll], axis=-1)
    ost_s[0, rows * half_heads:, :] = ml[:half_heads]
    ost_s[1, rows * half_heads:, :] = ml[half_heads:]
    st_copy().start()

    ph('stat_wait')
    st_copy().wait_recv()
    ph('merge')
    base = rows * half_heads
    m_s, l_s = ost_s[c, base:, :HALF], ost_s[c, base:, HALF:]
    m_p, l_p = orx_s[base:, :HALF], orx_s[base:, HALF:]
    m_c = jnp.maximum(m_s, m_p)
    w_own, w_par = jnp.exp(m_s - m_c), jnp.exp(m_p - m_c)

    def put(at, val):
        cz_s[pl.ds(at, half_heads, stride=chunk), :] = val

    for b in range(rows):
        sl = slice(b * half_heads, (b + 1) * half_heads)
        mix = ost_s[c, sl, :] * w_own[:, b:b + 1] + orx_s[sl, :] * w_par[:, b:b + 1]
        at = b if b < hr else hi_at + b - hr
        put(at, mix[:, :HALF])
        put(at + hr, mix[:, HALF:])
    put(ml_at, m_c)
    put(ml_at + 1, l_s * w_own + l_p * w_par)
    nil = jnp.zeros((half_heads, HALF), F32)
    for i in range(2, 8):
        put(ml_at + i, nil)
    for i in (0, 1, 2, 3, 6, 7):
        aa_copy(i).start()

    row_lane = lax.broadcasted_iota(jnp.int32, (1, HALF), 1)
    is_lo = row_lane < hr

    def blend(parts, out):
        ms, ls = [], []
        for ref, at, lo, hi in parts:
            m, l = ref[at:at + 1, :], ref[at + 1:at + 2, :]
            if lo is None:
                m, l = jnp.where(is_lo, NEG_FILL, m), jnp.where(is_lo, 0.0, l)
            if hi is None:
                m, l = jnp.where(is_lo, m, NEG_FILL), jnp.where(is_lo, l, 0.0)
            ms.append(m)
            ls.append(l)
        top = functools.reduce(jnp.maximum, ms)
        ws = [jnp.exp(m - top) for m in ms]
        l_sum = functools.reduce(lambda a, b: a + b, [l * w for l, w in zip(ls, ws)])
        pad = [jnp.zeros_like(top)] * (8 - len(parts) - 1)
        cols = jnp.transpose(jnp.concatenate(ws + [l_sum] + pad, axis=0))
        for half in range(2):
            for t in range(2):
                acc = None
                for j, (ref, at, lo, hi) in enumerate(parts):
                    off = (lo, hi)[half]
                    if off is None:
                        continue
                    term = ref[off + t * hr:off + (t + 1) * hr, :] * cols[half * hr:(half + 1) * hr, j:j + 1]
                    acc = term if acc is None else acc + term
                out(half, t, acc, cols[half * hr:(half + 1) * hr, len(parts):len(parts) + 1])
        return top, l_sum

    ph('aa_wait')
    for i in range(4):
        aa_copy(i).wait_recv()
    ph('aa_add')
    for side, k in ((0, 2), (1, -2)):
        half_part = (ta_s.at[2], ml_at, 0, None) if side == 0 else (ta_s.at[3], 0, None, 8)

        def keep(half, t, acc, _, side=side):
            off = (0, hi_at)[half] + t * hr
            tw_s[side, off:off + hr, :] = acc

        top, l_sum = blend([(cz_at(k, 0, chunk), ml_at, 0, hi_at), (ta_s.at[side], ml_at, 0, hi_at), half_part], keep)
        tw_s[side, ml_at:ml_at + 8, :] = jnp.concatenate([top, l_sum, jnp.zeros((6, HALF), F32)], axis=0)
        aa_copy(4 + side).start()

    ph('ma_on')
    ma_wait(0)
    ma_wait(1)
    for i in range(4, 8):
        ma_copy(i).start()
    ma_wait(2)
    ma_wait(3)
    for k in (2, -2, 1, -1):
        ma_fwd(c, k).start()

    ph('aa_wait2')
    for i in range(4, 8):
        aa_copy(i).wait_recv()
    ph('context')

    def finish(half, t, acc, l_col):
        g_s[c * chips + z, half * hr:(half + 1) * hr, t * HALF:(t + 1) * HALF] = (acc / l_col).astype(BF16).astype(F32)

    blend([(cz_at(0, 0, chunk), ml_at, 0, hi_at)] + [(tb_s.at[j], ml_at, 0, hi_at) for j in range(4)], finish)
    for i in range(4):
        cg_copy(i).start()
    cg_fwd(c, 0).start()

    ph('wo_wait')
    for i in range(n_col):
        wo_copy(i).wait()

    def out_dots(todo, first=False):
        lhs = [g_s[slot].astype(BF16) for slot in todo]
        for n in range(n_col):
            acc = None
            for slot, a in zip(todo, lhs):
                w = w_s[pl.ds(pl.multiple_of(n * d_model + slot * BLK, BLK), BLK), :]
                p = jnp.dot(a, w, preferred_element_type=F32)
                acc = p if acc is None else acc + p
            sl = slice(n * BLK, (n + 1) * BLK)
            acc_s[:, sl] = acc if first else acc_s[:, sl] + acc

    def mine(k):
        return c * chips + chip(k)

    def theirs(k):
        return pc * chips + chip(k)

    ph('out_0')
    out_dots([mine(0)], True)
    ph('ma_tail')
    for i in range(4, 8):
        ma_wait(i)
    for k in (3, -3, 4):
        ma_fwd(c, k).start()
    ph('cg_wait0')
    cg_fwd(pc, 0).wait_recv()
    cg_wait(0)
    cg_copy(4).start()
    cg_copy(6).start()
    cg_fwd(c, -2).start()
    cg_wait(1)
    cg_copy(5).start()
    cg_copy(7).start()
    cg_fwd(c, 2).start()
    ph('out_1')
    out_dots([theirs(0), mine(-2), mine(2)])
    ph('cg_wait1')
    cg_wait(2)
    cg_fwd(c, -1).start()
    cg_wait(3)
    cg_fwd(c, 1).start()
    ph('out_2')
    out_dots([mine(-1), mine(1)])
    ph('cg_wait2')
    cg_fwd(pc, -2).wait_recv()
    cg_fwd(pc, 2).wait_recv()
    ph('out_3')
    out_dots([theirs(-2), theirs(2)])
    ph('cg_wait3')
    cg_wait(4)
    cg_fwd(c, -3).start()
    cg_wait(5)
    cg_fwd(c, 3).start()
    cg_fwd(pc, -1).wait_recv()
    cg_fwd(pc, 1).wait_recv()
    ph('out_4')
    out_dots([mine(-3), mine(3), theirs(-1), theirs(1)])
    ph('cg_wait4')
    cg_wait(6)
    cg_wait(7)
    cg_fwd(c, 4).start()
    ph('out_5')
    out_dots([mine(4)])
    ph('cg_wait5')
    cg_fwd(pc, -3).wait_recv()
    cg_fwd(pc, 3).wait_recv()
    cg_fwd(pc, 4).wait_recv()
    ph('out_6')
    out_dots([theirs(-3), theirs(3), theirs(4)])
    ph('final')
    for k in range(chips):
        ma_fwd(pc, k).wait_recv()
    for n in range(n_col):
        sl = slice(n * BLK, (n + 1) * BLK)
        out_ref[:, sl] = (x_s[:, sl].astype(F32) + acc_s[:, sl] + ma_s[n]).astype(BF16)

    ph('drain')
    for i in range(chips):
        pd_copy(i).wait_send()
        ma_fwd(c, i).wait_send()
        cg_fwd(c, i).wait_send()
    for i in range(8):
        rs_copy(i).wait_send()
        aa_copy(i).wait_send()
        ma_copy(i).wait_send()
        cg_copy(i).wait_send()
    for i in range(slots):
        qx_copy(c, i).wait_send()
    st_copy().wait_send()
    ph(None)


def device_step(n_sp, hidden, ln_gamma, ln_beta, w_qkv, w_out, w_up, w_down, k_cache, v_cache, positions):
    rows, d_model = hidden.shape
    seq, head_dim = k_cache.shape[1], k_cache.shape[2]
    heads = w_out.shape[0] // head_dim
    ff = w_up.shape[1]
    chips = n_sp // 2
    slots = (heads + 2) // 2
    assert head_dim == BLK and heads == n_sp and d_model == n_sp * BLK and chips == 8
    inv_freq = 1.0 / (ROPE_BASE ** (jnp.arange(0, head_dim, 2, dtype=F32) / head_dim))
    local_pos = positions - lax.axis_index('sp') * seq
    n_up, n_col = ff // BLK, d_model // BLK
    w_rows = n_up * d_model + n_col * ff + slots * d_model
    n_kv = 3
    half = heads // 2
    any_spec = pl.BlockSpec(memory_space=pl.ANY)
    vmem_spec = pl.BlockSpec(memory_space=pltpu.VMEM)
    dma = pltpu.SemaphoreType.DMA
    hr = rows // 2
    chunk, part = 4 * hr + 8, 2 * hr + 8
    scratch = [
        pltpu.VMEM((rows, d_model), BF16),
        pltpu.VMEM((16, d_model), F32),
        pltpu.VMEM((rows, d_model), BF16),
        pltpu.VMEM((rows, ff), BF16),
        pltpu.VMEM((w_rows, BLK), BF16),
        pltpu.VMEM(k_cache.shape, BF16),
        pltpu.VMEM(v_cache.shape, BF16),
        pltpu.SMEM((rows,), jnp.int32),
        pltpu.VMEM((rows, HALF), F32),
        pltpu.VMEM((rows, HALF), F32),
        pltpu.VMEM((rows, HALF), F32),
        pltpu.VMEM(((heads + 2) * 2 * rows, HALF), F32),
        pltpu.VMEM((chips, rows, BLK), F32),
        pltpu.VMEM((chips, rows, BLK), F32),
        pltpu.VMEM((chips, rows, BLK), F32),
        pltpu.VMEM((3, rows, BLK), F32),
        pltpu.VMEM((4, rows, BLK), F32),
        pltpu.VMEM((n_sp, rows, BLK), F32),
        pltpu.VMEM((2, (rows + 1) * half, BLK), F32),
        pltpu.VMEM(((rows + 1) * half, BLK), F32),
        pltpu.VMEM((chips * chunk, HALF), F32),
        pltpu.VMEM((4, chunk, HALF), F32),
        pltpu.VMEM((4, chunk, HALF), F32),
        pltpu.VMEM((2, chunk, HALF), F32),
        pltpu.VMEM((n_sp, rows, BLK), F32),
        pltpu.VMEM((rows, d_model), F32),
        dma((4,)), dma((n_up,)), dma((n_col,)), dma((slots,)), dma((2, n_kv)), dma((n_col,)),
        dma((chips,)), dma((chips,)), dma((slots,)), dma((slots,)), dma((1,)), dma((1,)),
    ] + [dma((8,))] * 12
    out, k_new, v_new = pl.pallas_call(
        functools.partial(layer_kernel, chips, heads),
        out_shape=(jax.ShapeDtypeStruct((rows, d_model), BF16), jax.ShapeDtypeStruct((rows, BLK), BF16), jax.ShapeDtypeStruct((rows, BLK), BF16)),
        in_specs=[any_spec] * 10 + [vmem_spec],
        out_specs=(vmem_spec, vmem_spec, vmem_spec),
        scratch_shapes=scratch,
        compiler_params=pltpu.CompilerParams(collective_id=0, has_side_effects=True, vmem_limit_bytes=63 * 1024 * 1024),
        name='decode_layer',
    )(hidden, ln_gamma.reshape(1, -1), ln_beta.reshape(1, -1), w_qkv, w_out, w_up, w_down, k_cache, v_cache, positions, inv_freq.reshape(1, -1))
    write_mask = (jnp.arange(seq)[None, :] == local_pos[:, None])[:, :, None]
    k_next = jnp.where(write_mask, k_new[:, None, :], k_cache)
    v_next = jnp.where(write_mask, v_new[:, None, :], v_cache)
    return out, k_next, v_next


def solution(mesh):
    cache_spec = P('dp', 'sp', None)
    in_specs = (P('dp', None), P(None), P(None), P(None, None), P(None, None), P(None, 'sp'), P('sp', None), cache_spec, cache_spec, P('dp'))
    out_specs = (P('dp', None), cache_spec, cache_spec)
    return jax.shard_map(functools.partial(device_step, mesh.shape['sp']), mesh=mesh, in_specs=in_specs, out_specs=out_specs, check_vma=False)
```

time: 86.2 us -> 62.3 us (0.72)
  Pallas kernels: 75.5 us -> 52.7 us
    pallas_call x1, Pallas kernels: 75.5 us -> 52.7 us  [device_step(): pl.pallas_call(functools.partial(layer_kernel, chips, heads), out_shape=(...]
where the time goes in v2:
time: 62.3 us; the launch traced here: 62.1 us
  Pallas kernels  52.7 us (85%)
  other arithmetic  8.04 us (13%)
  local copies, waits for them, and re-layouts  0.75 us (1%)
  between operations  0.65 us (1%)
    pallas_call x1, Pallas kernels, device_step(): pl.pallas_call(functools.partial(layer_kernel, chips, heads), out_shape=(...  52.7 us
    select_n x1, other arithmetic, device_step(): v_next = jnp.where(write_mask, v_new[:, None, :], v_cache)  6.78 us

profile of v2, /device:TPU:21, one launch (start us, length us, event | category | flops | bytes accessed | tf_op | source)
XLA Modules:
  0.0 62.1 jit_solution(1195816134652243413)
XLA Ops:
  0.6 0.7 %broadcast_subtract_fusion = s32[48]{0:T(128)S(1)} fusion(s32[48]{0:T(128)} %pos_hbm.1, s32[]{:T(128)S(6)} %mul.6), kind=kLoop, calls=%fused_computation.4 | loop fusion | flops 48 | bytes 388 | tf_op jit(solution)/shard_map/sub | solution.py:566
  1.3 0.5 negate_power_fusion.inv_ref
  1.8 0.1 iota_compare_fusion
  1.9 52.7 %decode_layer.1 = (bf16[48,4096]{1,0:T(8,128)(2,1)}, bf16[48,256]{1,0:T(8,128)(2,1)}, bf16[48,256]{1,0:T(8,128)(2,1)}) custom-call(bf16[48,4096]{1,0:T(8,128)(2,1)} %x_hbm.1, f32[1,4096]{1,0:T(1,128)} %bitcast.2, f32[1,4096]{1,0:T(1,128)} %bitcast.3, bf16[4096,4608]{1,0:T(8,128)(2,1)} %wqkv_hbm.1, bf16[4096,4096]{1,0:T(8,128)(2,1)} %wout_hbm.1, ...), custom_call_target="tpu_custom_call" | custom-call | tf_op jit(solution)/shard_map/decode_layer/pallas_call | solution.py:606
  54.6 0.0 copy-start
  54.6 6.8 %broadcast_select_fusion = (bf16[48,128,256]{2,1,0:T(8,128)(2,1)}, bf16[48,128,256]{2,1,0:T(8,128)(2,1)}) fusion(bf16[48,128,256]{2,1,0:T(8,128)(2,1)} %v_hbm.1, pred[48,128]{1,0:T(8,128)(4,1)S(1)} %iota_compare_fusion, bf16[48,256]{1,0:T(8,128)(2,1)} %get-tuple-element.8, bf16[48,128,256]{2,1,0:T(8,128)(2,1)} %k_hbm.1, bf16[48,256]{1,0:T(8,128)(2,1)} %get-tuple-element.7), kind=kLoop, calls=%fused_computation | loop fusion | flops 3145728 | bytes 12638208 | tf_op jit(solution)/shard_map/jit(_where)/select_n | solution.py:617
  61.4 0.0 copy-done
  61.4 0.7 %copy.14 = bf16[48,4096]{1,0:T(8,128)(2,1)} copy(bf16[48,4096]{1,0:T(8,128)(2,1)S(1)} %copy-done) | data formatting | bytes 786432
Async XLA Ops:
  54.6 6.8 %copy-start = (bf16[48,4096]{1,0:T(8,128)(2,1)S(1)}, bf16[48,4096]{1,0:T(8,128)(2,1)}, u32[]{:S(2)}) copy-start(bf16[48,4096]{1,0:T(8,128)(2,1)} %get-tuple-element.14) | copy-start | bytes 1179652

commit v3 on v2

--- a/solution.py
+++ b/solution.py
@@ -33,8 +33,8 @@
 
 
 def layer_kernel(chips, heads, x_hbm, gamma_hbm, beta_hbm, wqkv_hbm, wout_hbm, wup_hbm, wdown_hbm, k_hbm, v_hbm, pos_hbm,
-                 inv_ref, out_ref, knew_ref, vnew_ref,
-                 x_s, gb_s, h_s, act_s, w_s, k_s, v_s, pos_s, lp_s, cs_s, sn_s, qk_s,
+                 inv_ref, out_ref, k_s, v_s,
+                 x_s, gb_s, h_s, act_s, w_s, pos_s, lp_s, cs_s, sn_s, qk_s,
                  ps_s, pr_s, ss_s, ra_s, rb_s, ma_s, ost_s, orx_s, cz_s, ta_s, tb_s, tw_s, g_s, acc_s,
                  in_sem, up_sem, dn_sem, qkv_sem, kv_sem, wo_sem,
                  pd_send, pd_recv, qx_send, qx_recv, st_send, st_recv,
@@ -169,24 +169,21 @@
     ph('entry')
     for i in range(4):
         in_copy(i).start()
-    for i in range(n_up):
+    for i in range(2):
         up_copy(i).start()
     bar = pltpu.get_barrier_semaphore()
     pl.semaphore_signal(bar, inc=1, device_id=partner, device_id_type=MESH)
     for k in (1, -1, 2, -2):
         pl.semaphore_signal(bar, inc=1, device_id=peer(k), device_id_type=MESH)
+
+    ph('in_wait')
+    for i in range(4):
+        in_copy(i).wait()
+    for i in range(2, n_up):
+        up_copy(i).start()
     for half in range(2):
         for i in range(chips):
             dn_copy(half, i).start()
-    for i in range(slots):
-        qkv_copy(i).start()
-    for i in range(n_kv):
-        kv_copy(0, i).start()
-        kv_copy(1, i).start()
-
-    ph('in_wait')
-    for i in range(4):
-        in_copy(i).wait()
     ph('layer_norm')
 
     @pl.loop(0, rows // 16)
@@ -218,30 +215,35 @@
 
     ph('mlp_up')
 
-    @pl.loop(0, n_up // 2)
-    def _(i):
-        up_copy(2 * i).wait()
-        up_copy(2 * i + 1).wait()
-        us = chunk_dots(h_s, [(2 * i + j) * up_rows for j in range(2)], up_rows)
+    for i in range(0, n_up, 2):
+        up_copy(i).wait()
+        up_copy(i + 1).wait()
+        us = chunk_dots(h_s, [(i + j) * up_rows for j in range(2)], up_rows)
         for j, u in enumerate(us):
             g = 0.5 * u * (1.0 + lax.erf(u * (0.5 ** 0.5)))
-            act_s[:, pl.ds(pl.multiple_of((2 * i + j) * BLK, BLK), BLK)] = g.astype(BF16)
+            act_s[:, (i + j) * BLK:(i + j + 1) * BLK] = g.astype(BF16)
+        if i == 0:
+            for n in range(3):
+                qkv_copy(n).start()
 
     ph('barrier')
     pl.semaphore_wait(bar, 5)
     ph('down_partner')
-    for i in range(0, chips, 2):
-        for j in range(2):
+    qkv_copy(3).start()
+    for i in range(0, chips, 4):
+        for j in range(4):
             dn_copy(0, i + j).wait()
-        for j, p in enumerate(chunk_dots(act_s, [dn_base + (i + j) * dn_rows for j in range(2)], dn_rows)):
+        for j, p in enumerate(chunk_dots(act_s, [dn_base + (i + j) * dn_rows for j in range(4)], dn_rows)):
             ps_s[i + j] = p
             pd_copy(i + j).start()
 
     ph('down_own')
-    for i in range(0, chips, 2):
-        for j in range(2):
+    for i in range(4, 6):
+        qkv_copy(i).start()
+    for i in range(0, chips, 4):
+        for j in range(4):
             dn_copy(1, i + j).wait()
-        for j, p in enumerate(chunk_dots(act_s, [dn_base + (chips + i + j) * dn_rows for j in range(2)], dn_rows)):
+        for j, p in enumerate(chunk_dots(act_s, [dn_base + (chips + i + j) * dn_rows for j in range(4)], dn_rows)):
             n = i + j
             pd_copy(n).wait_recv()
             ss_s[n] = p + pr_s[n]
@@ -269,7 +271,13 @@
 
     n_pair = slots // 2
     ph('qkv')
+    for i in range(6, slots):
+        qkv_copy(i).start()
     pl.loop(0, n_pair - 1)(qkv_pair)
+
+    for i in range(n_kv):
+        kv_copy(0, i).start()
+        kv_copy(1, i).start()
 
     ph('rs_add')
     for i in range(4):
@@ -292,11 +300,6 @@
     ph('qkv_wait')
     for i in range(slots):
         qx_copy(pc, i).wait_recv()
-    for t in range(2):
-        sl = slice(t * HALF, (t + 1) * HALF)
-        knew_ref[:, sl] = qk_s[(2 * heads + t) * rows:(2 * heads + t + 1) * rows, :].astype(BF16)
-        vnew_ref[:, sl] = qk_s[(2 * heads + 2 + t) * rows:(2 * heads + 3 + t) * rows, :].astype(BF16)
-
     lane = lax.broadcasted_iota(jnp.int32, (heads, seq), 1)
     lane_f = lane.astype(F32)
     scale = k_s.shape[2] ** -0.5
@@ -387,7 +390,7 @@
     nil = jnp.zeros((half_heads, HALF), F32)
     for i in range(2, 8):
         put(ml_at + i, nil)
-    for i in (0, 1, 2, 3, 6, 7):
+    for i in (2, 3, 0, 1):
         aa_copy(i).start()
 
     row_lane = lax.broadcasted_iota(jnp.int32, (1, HALF), 1)
@@ -420,21 +423,19 @@
                 out(half, t, acc, cols[half * hr:(half + 1) * hr, len(parts):len(parts) + 1])
         return top, l_sum
 
-    ph('aa_wait')
-    for i in range(4):
-        aa_copy(i).wait_recv()
-    ph('aa_add')
-    for side, k in ((0, 2), (1, -2)):
-        half_part = (ta_s.at[2], ml_at, 0, None) if side == 0 else (ta_s.at[3], 0, None, 8)
-
-        def keep(half, t, acc, _, side=side):
-            off = (0, hi_at)[half] + t * hr
-            tw_s[side, off:off + hr, :] = acc
-
-        top, l_sum = blend([(cz_at(k, 0, chunk), ml_at, 0, hi_at), (ta_s.at[side], ml_at, 0, hi_at), half_part], keep)
-        tw_s[side, ml_at:ml_at + 8, :] = jnp.concatenate([top, l_sum, jnp.zeros((6, HALF), F32)], axis=0)
-        aa_copy(4 + side).start()
-
+    slot_f = lax.broadcasted_iota(jnp.int32, (seq, HALF), 0).astype(F32)
+
+    def insert(ref, head):
+        @pl.loop(0, rows)
+        def _(b):
+            hit = slot_f == lp_s[pl.ds(b, 1), :]
+            for t in range(2):
+                new = qk_s[pl.ds((2 * head + t) * rows + b, 1), :]
+                sl = slice(t * HALF, (t + 1) * HALF)
+                ref[b, :, sl] = jnp.where(hit, new, ref[b, :, sl].astype(F32)).astype(BF16)
+
+    ph('insert_k')
+    insert(k_s, heads)
     ph('ma_on')
     ma_wait(0)
     ma_wait(1)
@@ -445,6 +446,25 @@
     for k in (2, -2, 1, -1):
         ma_fwd(c, k).start()
 
+    for i in (6, 7):
+        aa_copy(i).start()
+    ph('aa_wait')
+    for i in range(4):
+        aa_copy(i).wait_recv()
+    ph('aa_add')
+    for side, k in ((0, 2), (1, -2)):
+        half_part = (ta_s.at[2], ml_at, 0, None) if side == 0 else (ta_s.at[3], 0, None, 8)
+
+        def keep(half, t, acc, _, side=side):
+            off = (0, hi_at)[half] + t * hr
+            tw_s[side, off:off + hr, :] = acc
+
+        top, l_sum = blend([(cz_at(k, 0, chunk), ml_at, 0, hi_at), (ta_s.at[side], ml_at, 0, hi_at), half_part], keep)
+        tw_s[side, ml_at:ml_at + 8, :] = jnp.concatenate([top, l_sum, jnp.zeros((6, HALF), F32)], axis=0)
+        aa_copy(4 + side).start()
+
+    ph('insert_v')
+    insert(v_s, heads + 1)
     ph('aa_wait2')
     for i in range(4, 8):
         aa_copy(i).wait_recv()
@@ -481,56 +501,54 @@
 
     ph('out_0')
     out_dots([mine(0)], True)
+    ph('cg_wait0')
+    cg_fwd(pc, 0).wait_recv()
+    ph('out_0b')
+    out_dots([theirs(0)])
+    ph('cg_wait1')
+    cg_wait(0)
+    cg_copy(6).start()
+    cg_copy(4).start()
+    cg_wait(1)
+    cg_copy(7).start()
+    cg_copy(5).start()
+    cg_fwd(c, -2).start()
+    cg_fwd(c, 2).start()
+    cg_wait(2)
+    cg_fwd(c, -1).start()
+    cg_wait(3)
+    cg_fwd(c, 1).start()
+    ph('out_1')
+    out_dots([mine(-2), mine(2), mine(-1), mine(1)])
     ph('ma_tail')
     for i in range(4, 8):
         ma_wait(i)
     for k in (3, -3, 4):
         ma_fwd(c, k).start()
-    ph('cg_wait0')
-    cg_fwd(pc, 0).wait_recv()
-    cg_wait(0)
-    cg_copy(4).start()
-    cg_copy(6).start()
-    cg_fwd(c, -2).start()
-    cg_wait(1)
-    cg_copy(5).start()
-    cg_copy(7).start()
-    cg_fwd(c, 2).start()
-    ph('out_1')
-    out_dots([theirs(0), mine(-2), mine(2)])
-    ph('cg_wait1')
-    cg_wait(2)
-    cg_fwd(c, -1).start()
-    cg_wait(3)
-    cg_fwd(c, 1).start()
+    ph('cg_wait2')
+    for k in (-2, 2, -1, 1):
+        cg_fwd(pc, k).wait_recv()
     ph('out_2')
-    out_dots([mine(-1), mine(1)])
-    ph('cg_wait2')
-    cg_fwd(pc, -2).wait_recv()
-    cg_fwd(pc, 2).wait_recv()
-    ph('out_3')
-    out_dots([theirs(-2), theirs(2)])
+    out_dots([theirs(-2), theirs(2), theirs(-1), theirs(1)])
     ph('cg_wait3')
     cg_wait(4)
     cg_fwd(c, -3).start()
     cg_wait(5)
     cg_fwd(c, 3).start()
-    cg_fwd(pc, -1).wait_recv()
-    cg_fwd(pc, 1).wait_recv()
-    ph('out_4')
-    out_dots([mine(-3), mine(3), theirs(-1), theirs(1)])
+    ph('out_3')
+    out_dots([mine(-3), mine(3)])
     ph('cg_wait4')
     cg_wait(6)
     cg_wait(7)
     cg_fwd(c, 4).start()
-    ph('out_5')
-    out_dots([mine(4)])
-    ph('cg_wait5')
     cg_fwd(pc, -3).wait_recv()
     cg_fwd(pc, 3).wait_recv()
+    ph('out_4')
+    out_dots([mine(4), theirs(-3), theirs(3)])
+    ph('cg_wait5')
     cg_fwd(pc, 4).wait_recv()
-    ph('out_6')
-    out_dots([theirs(-3), theirs(3), theirs(4)])
+    ph('out_5')
+    out_dots([theirs(4)])
     ph('final')
     for k in range(chips):
         ma_fwd(pc, k).wait_recv()
@@ -554,6 +572,21 @@
     ph(None)
 
 
+def store_kernel(*refs):
+    srcs, dsts, sem = refs[:3], refs[3:6], refs[6]
+    copies = []
+    for n, (src, dst) in enumerate(zip(srcs, dsts)):
+        parts = 1 if n == 0 else 4
+        step = src.shape[0] // parts
+        for i in range(parts):
+            sl = pl.ds(i * step, step)
+            copies.append(pltpu.make_async_copy(src.at[sl], dst.at[sl], sem.at[n, i]))
+    for copy in copies:
+        copy.start()
+    for copy in copies:
+        copy.wait()
+
+
 def device_step(n_sp, hidden, ln_gamma, ln_beta, w_qkv, w_out, w_up, w_down, k_cache, v_cache, positions):
     rows, d_model = hidden.shape
     seq, head_dim = k_cache.shape[1], k_cache.shape[2]
@@ -563,12 +596,11 @@
     slots = (heads + 2) // 2
     assert head_dim == BLK and heads == n_sp and d_model == n_sp * BLK and chips == 8
     inv_freq = 1.0 / (ROPE_BASE ** (jnp.arange(0, head_dim, 2, dtype=F32) / head_dim))
-    local_pos = positions - lax.axis_index('sp') * seq
     n_up, n_col = ff // BLK, d_model // BLK
     w_rows = n_up * d_model + n_col * ff + slots * d_model
     n_kv = 3
     half = heads // 2
-    any_spec = pl.BlockSpec(memory_space=pl.ANY)
+    any_spec = pl.BlockSpec(memory_space=pltpu.HBM)
     vmem_spec = pl.BlockSpec(memory_space=pltpu.VMEM)
     dma = pltpu.SemaphoreType.DMA
     hr = rows // 2
@@ -579,8 +611,6 @@
         pltpu.VMEM((rows, d_model), BF16),
         pltpu.VMEM((rows, ff), BF16),
         pltpu.VMEM((w_rows, BLK), BF16),
-        pltpu.VMEM(k_cache.shape, BF16),
-        pltpu.VMEM(v_cache.shape, BF16),
         pltpu.SMEM((rows,), jnp.int32),
         pltpu.VMEM((rows, HALF), F32),
         pltpu.VMEM((rows, HALF), F32),
@@ -603,19 +633,25 @@
         dma((4,)), dma((n_up,)), dma((n_col,)), dma((slots,)), dma((2, n_kv)), dma((n_col,)),
         dma((chips,)), dma((chips,)), dma((slots,)), dma((slots,)), dma((1,)), dma((1,)),
     ] + [dma((8,))] * 12
-    out, k_new, v_new = pl.pallas_call(
+    in_hbm = [pltpu.with_memory_space_constraint(a, pltpu.HBM) for a in (hidden, ln_gamma.reshape(1, -1), ln_beta.reshape(1, -1))]
+    results = pl.pallas_call(
         functools.partial(layer_kernel, chips, heads),
-        out_shape=(jax.ShapeDtypeStruct((rows, d_model), BF16), jax.ShapeDtypeStruct((rows, BLK), BF16), jax.ShapeDtypeStruct((rows, BLK), BF16)),
+        out_shape=(pltpu.VMEM(hidden.shape, BF16), pltpu.VMEM(k_cache.shape, BF16), pltpu.VMEM(v_cache.shape, BF16)),
         in_specs=[any_spec] * 10 + [vmem_spec],
         out_specs=(vmem_spec, vmem_spec, vmem_spec),
         scratch_shapes=scratch,
-        compiler_params=pltpu.CompilerParams(collective_id=0, has_side_effects=True, vmem_limit_bytes=63 * 1024 * 1024),
+        compiler_params=pltpu.CompilerParams(collective_id=0, has_side_effects=True, vmem_limit_bytes=46 * 1024 * 1024),
         name='decode_layer',
-    )(hidden, ln_gamma.reshape(1, -1), ln_beta.reshape(1, -1), w_qkv, w_out, w_up, w_down, k_cache, v_cache, positions, inv_freq.reshape(1, -1))
-    write_mask = (jnp.arange(seq)[None, :] == local_pos[:, None])[:, :, None]
-    k_next = jnp.where(write_mask, k_new[:, None, :], k_cache)
-    v_next = jnp.where(write_mask, v_new[:, None, :], v_cache)
-    return out, k_next, v_next
+    )(*in_hbm, w_qkv, w_out, w_up, w_down, k_cache, v_cache, pltpu.with_memory_space_constraint(positions, pltpu.HBM), inv_freq.reshape(1, -1))
+    return pl.pallas_call(
+        store_kernel,
+        out_shape=[jax.ShapeDtypeStruct(r.shape, r.dtype) for r in results],
+        in_specs=[vmem_spec] * 3,
+        out_specs=[pl.BlockSpec(memory_space=pltpu.HBM)] * 3,
+        scratch_shapes=[dma((3, 4))],
+        compiler_params=pltpu.CompilerParams(vmem_limit_bytes=1024 * 1024),
+        name='store_results',
+    )(*results)
 
 
 def solution(mesh):

time: 62.3 us -> 53.6 us (0.86)
  other arithmetic: 8.04 us -> 0.01 us
  local copies, waits for them, and re-layouts: 0.75 us -> 0 us
    select_n x1 -> x0, other arithmetic: 6.78 us -> none  [device_step(): v_next = jnp.where(write_mask, v_new[:, None, :], v_cache)]
    pallas_call x0 -> x1, Pallas kernels: none -> 2.88 us  [device_step(): pl.pallas_call(store_kernel, out_shape=[jax.ShapeDtypeStruct(r.shape, r.d...]
    pallas_call x1, Pallas kernels: 52.7 us -> 50 us  [device_step(): pl.pallas_call(functools.partial(layer_kernel, chips, heads), out_shape=(...]
    unnamed x3 -> x0, local copies, waits for them, and re-layouts: 0.75 us -> none
    sub x1 -> x0, other arithmetic: 0.66 us -> none  [device_step(): local_pos = positions - lax.axis_index('sp') * seq]
where the time goes in v3:
time: 53.6 us; the launch traced here: 53.5 us
  Pallas kernels  52.8 us (99%)
  between operations  0.64 us (1%)
    pallas_call x1, Pallas kernels, device_step(): pl.pallas_call(functools.partial(layer_kernel, chips, heads), out_shape=(...  50 us
    pallas_call x1, Pallas kernels, device_step(): pl.pallas_call(store_kernel, out_shape=[jax.ShapeDtypeStruct(r.shape, r.d...  2.88 us

profile of v3, /device:TPU:21, one launch (start us, length us, event | category | flops | bytes accessed | tf_op | source)
XLA Modules:
  0.0 53.5 jit_solution(9245264503614550559)
XLA Ops:
  0.6 50.0 %decode_layer.1 = (bf16[48,4096]{1,0:T(8,128)(2,1)S(1)}, bf16[48,128,256]{2,1,0:T(8,128)(2,1)S(1)}, bf16[48,128,256]{2,1,0:T(8,128)(2,1)S(1)}) custom-call(bf16[48,4096]{1,0:T(8,128)(2,1)} %x_hbm.1, f32[1,4096]{1,0:T(1,128)} %bitcast.2, f32[1,4096]{1,0:T(1,128)} %bitcast.3, bf16[4096,4608]{1,0:T(8,128)(2,1)} %wqkv_hbm.1, bf16[4096,4096]{1,0:T(8,128)(2,1)} %wout_hbm.1, ...), custom_call_target="tpu_custom_call" | custom-call | tf_op jit(solution)/shard_map/decode_layer/pallas_call | solution.py:637
  50.6 2.9 %store_results.1 = (bf16[48,4096]{1,0:T(8,128)(2,1)}, bf16[48,128,256]{2,1,0:T(8,128)(2,1)}, bf16[48,128,256]{2,1,0:T(8,128)(2,1)}) custom-call(bf16[48,4096]{1,0:T(8,128)(2,1)S(1)} %get-tuple-element.6.refs_0_, bf16[48,128,256]{2,1,0:T(8,128)(2,1)S(1)} %get-tuple-element.7.refs_1_, bf16[48,128,256]{2,1,0:T(8,128)(2,1)S(1)} %get-tuple-element.8.refs_2_), custom_call_target="tpu_custom_call" | custom-call | tf_op jit(solution)/shard_map/store_results/pallas_call | solution.py:646
  (1 shorter events, 0.0 us)

commit v4 on v3

--- a/solution.py
+++ b/solution.py
@@ -48,9 +48,8 @@
     slots = (heads + 2) // 2
     hr = rows // 2
     ml_at = 2 * hr
-    hi_at = ml_at + 8
-    chunk = 4 * hr + 8
-    part = 2 * hr + 8
+    chunk = 2 * hr + 8
+    top_rows = hr * half_heads
     up_rows, dn_rows = d_model, ff
     dn_base = n_up * up_rows
     qkv_base = dn_base + n_col * dn_rows
@@ -111,8 +110,8 @@
         ref = qk_s.at[pl.ds(row, 2 * rows)]
         return remote(ref, ref, qx_send.at[i], qx_recv.at[i], partner)
 
-    def st_copy():
-        return remote(ost_s.at[pc], orx_s, st_send.at[0], st_recv.at[0], partner)
+    def st_copy(h):
+        return remote(ost_s.at[pc, h], orx_s.at[h], st_send.at[h], st_recv.at[h], partner)
 
     hops = (1, -1, 2, -2, 2, -2, 1, -1)
 
@@ -121,14 +120,15 @@
         dst = (ra_s.at[0], ra_s.at[1], ra_s.at[2, pl.ds(0, hr)], ra_s.at[2, pl.ds(hr, hr)], rb_s.at[0], rb_s.at[1], rb_s.at[2], rb_s.at[3])[i]
         return remote(src, dst, rs_send.at[i], rs_recv.at[i], peer(hops[i]))
 
-    def cz_at(k, off, n):
-        return cz_s.at[pl.ds(pl.multiple_of(chip(k) * chunk + off, 8), n)]
-
-    def aa_copy(i):
-        src = (lambda: cz_at(3, 0, chunk), lambda: cz_at(-3, 0, chunk), lambda: cz_at(4, 0, part), lambda: cz_at(4, ml_at, part),
-               lambda: tw_s.at[0], lambda: tw_s.at[1], lambda: cz_at(1, 0, chunk), lambda: cz_at(-1, 0, chunk))[i]()
-        dst = (ta_s.at[0], ta_s.at[1], ta_s.at[2, pl.ds(0, part)], ta_s.at[3, pl.ds(0, part)], tb_s.at[0], tb_s.at[1], tb_s.at[2], tb_s.at[3])[i]
-        return remote(src, dst, aa_send.at[i], aa_recv.at[i], peer(hops[i]))
+    def cz_at(h, k):
+        return cz_s.at[pl.ds(pl.multiple_of((h * chips + chip(k)) * chunk, 8), chunk)]
+
+    def aa_copy(h, i):
+        src = (lambda: cz_at(h, 3), lambda: cz_at(h, -3), lambda: cz_at(h, 4), lambda: tw_s.at[h, 0], lambda: tw_s.at[h, 1],
+               lambda: cz_at(h, 1), lambda: cz_at(h, -1))[i]()
+        dst = ta_s.at[h, i] if i < 3 else tb_s.at[h, i - 3]
+        hop = (1, -1, (2, -2)[h], 2, -2, 1, -1)[i]
+        return remote(src, dst, aa_send.at[7 * h + i], aa_recv.at[7 * h + i], peer(hop))
 
     g_hop = (2, -2, 1, -1, 1, -1, 2, -2)
     g_src = (0, 0, 0, 0, -2, 2, -2, 2)
@@ -148,14 +148,23 @@
     def ma_copy(i):
         return gather_copy(ma_s, ma_send, ma_recv, i)
 
-    def cg_copy(i):
-        return gather_copy(g_s, cg_send, cg_recv, i)
+    def cg_route(h, i):
+        return ((0, 2), (0, -2), (0, 1), (0, -1), (-2, 1), (2, -1), ((-2, 2), (2, -2))[h])[i]
+
+    def cg_part(h, i, k, hop):
+        ref = g_s.at[c * chips + chip(k), pl.ds(h * hr, hr)]
+        return remote(ref, ref, cg_send.at[7 * h + i], cg_recv.at[7 * h + i], peer(hop))
+
+    def cg_copy(h, i):
+        src, hop = cg_route(h, i)
+        return cg_part(h, i, src, hop)
 
     def ma_wait(i):
         gather_recv(ma_s, ma_send, ma_recv, i).wait_recv()
 
-    def cg_wait(i):
-        gather_recv(g_s, cg_send, cg_recv, i).wait_recv()
+    def cg_wait(h, i):
+        src, hop = cg_route(h, i)
+        cg_part(h, i, src - hop, hop).wait_recv()
 
     def ma_fwd(owner, k):
         ref = ma_s.at[owner * chips + chip(k)]
@@ -170,7 +179,7 @@
     for i in range(4):
         in_copy(i).start()
     for i in range(2):
-        up_copy(i).start()
+        qkv_copy(i).start()
     bar = pltpu.get_barrier_semaphore()
     pl.semaphore_signal(bar, inc=1, device_id=partner, device_id_type=MESH)
     for k in (1, -1, 2, -2):
@@ -179,11 +188,8 @@
     ph('in_wait')
     for i in range(4):
         in_copy(i).wait()
-    for i in range(2, n_up):
-        up_copy(i).start()
-    for half in range(2):
-        for i in range(chips):
-            dn_copy(half, i).start()
+    for i in range(2, slots):
+        qkv_copy(i).start()
     ph('layer_norm')
 
     @pl.loop(0, rows // 16)
@@ -195,6 +201,10 @@
         var = jnp.mean(cen * cen, axis=-1, keepdims=True)
         h_s[sl, :] = (cen * lax.rsqrt(var + LN_EPS) * gb_s[0:1, :] + gb_s[8:9, :]).astype(BF16)
 
+    nil = jnp.zeros((half_heads, HALF), F32)
+    for h in range(2):
+        for i in range(ml_at + 2, chunk):
+            cz_s[pl.ds(h * chips * chunk + i, half_heads, stride=chunk), :] = nil
     ph('rope')
     for b in range(rows):
         lp_s[b:b + 1, :] = jnp.full((1, HALF), pos_s[b], jnp.int32).astype(F32)
@@ -213,44 +223,7 @@
                 accs[j] = p if accs[j] is None else accs[j] + p
         return accs
 
-    ph('mlp_up')
-
-    for i in range(0, n_up, 2):
-        up_copy(i).wait()
-        up_copy(i + 1).wait()
-        us = chunk_dots(h_s, [(i + j) * up_rows for j in range(2)], up_rows)
-        for j, u in enumerate(us):
-            g = 0.5 * u * (1.0 + lax.erf(u * (0.5 ** 0.5)))
-            act_s[:, (i + j) * BLK:(i + j + 1) * BLK] = g.astype(BF16)
-        if i == 0:
-            for n in range(3):
-                qkv_copy(n).start()
-
-    ph('barrier')
-    pl.semaphore_wait(bar, 5)
-    ph('down_partner')
-    qkv_copy(3).start()
-    for i in range(0, chips, 4):
-        for j in range(4):
-            dn_copy(0, i + j).wait()
-        for j, p in enumerate(chunk_dots(act_s, [dn_base + (i + j) * dn_rows for j in range(4)], dn_rows)):
-            ps_s[i + j] = p
-            pd_copy(i + j).start()
-
-    ph('down_own')
-    for i in range(4, 6):
-        qkv_copy(i).start()
-    for i in range(0, chips, 4):
-        for j in range(4):
-            dn_copy(1, i + j).wait()
-        for j, p in enumerate(chunk_dots(act_s, [dn_base + (chips + i + j) * dn_rows for j in range(4)], dn_rows)):
-            n = i + j
-            pd_copy(n).wait_recv()
-            ss_s[n] = p + pr_s[n]
-            for m in ((0,), (1,), (2, 3), (), (), (6,), (7,), ())[n]:
-                rs_copy(m).start()
-
-    def qkv_store(i, acc):
+    def qkv_store(i, acc, send=True):
         a = acc.astype(BF16).astype(F32)
         a1, a2 = a[:, :HALF], a[:, HALF:]
         cs, sn = cs_s[...], sn_s[...]
@@ -261,41 +234,33 @@
         row = pl.multiple_of(slot * 2 * rows, 8)
         qk_s[pl.ds(row, rows), :] = jnp.where(is_v, a1, r1)
         qk_s[pl.ds(row + rows, rows), :] = jnp.where(is_v, a2, r2)
-        qx_copy(c, i).start()
-
-    def qkv_pair(i):
+        if send:
+            qx_copy(c, i).start()
+
+    def qkv_pair(i, send=True):
         qkv_copy(2 * i).wait()
         qkv_copy(2 * i + 1).wait()
         for j, acc in enumerate(chunk_dots(h_s, [qkv_base + (2 * i + j) * d_model for j in range(2)], d_model)):
-            qkv_store(2 * i + j, acc)
+            qkv_store(2 * i + j, acc, send)
 
     n_pair = slots // 2
     ph('qkv')
-    for i in range(6, slots):
-        qkv_copy(i).start()
-    pl.loop(0, n_pair - 1)(qkv_pair)
-
+    qkv_pair(0, False)
+    ph('barrier')
+    pl.semaphore_wait(bar, 5)
+    ph('qkv2')
+    for i in range(2):
+        qx_copy(c, i).start()
+    pl.loop(1, n_pair - 1)(qkv_pair)
     for i in range(n_kv):
         kv_copy(0, i).start()
         kv_copy(1, i).start()
 
-    ph('rs_add')
-    for i in range(4):
-        rs_copy(i).wait_recv()
-    ss_s[3, 0:hr] = ss_s[3, 0:hr] + ra_s[0, 0:hr] + ra_s[2, 0:hr]
-    ss_s[3, hr:] = ss_s[3, hr:] + ra_s[0, hr:]
-    ss_s[4, 0:hr] = ss_s[4, 0:hr] + ra_s[1, 0:hr]
-    ss_s[4, hr:] = ss_s[4, hr:] + ra_s[1, hr:] + ra_s[2, hr:]
-    rs_copy(4).start()
-    rs_copy(5).start()
     ph('qkv_last')
     qkv_pair(n_pair - 1)
     for i in range(2 * n_pair, slots):
         qkv_copy(i).wait()
         qkv_store(i, chunk_dots(h_s, [qkv_base + i * d_model], d_model)[0])
-
-    for i in range(n_col):
-        wo_copy(i).start()
 
     ph('qkv_wait')
     for i in range(slots):
@@ -305,9 +270,11 @@
     scale = k_s.shape[2] ** -0.5
     group = rows // 4
 
-    def attend(g, carry):
+    def attend(h, g, carry):
         mm, ll = carry
         base = g * group
+        kv_copy(0, g).wait()
+        kv_copy(1, g).wait()
         scores, values, here = [], [], []
         for r in range(group):
             b = base + r
@@ -330,7 +297,7 @@
         for r in range(group):
             m = jnp.max(scores[r], axis=-1, keepdims=True)
             e = jnp.where(lane_f <= lp_s[pl.ds(base + r, 1), :], jnp.exp(scores[r] - m), 0.0)
-            col = lane == base + r
+            col = lane == base + r - h * hr
             mm = jnp.where(col, m, mm)
             ll = jnp.where(col, jnp.sum(e, axis=-1, keepdims=True), ll)
             eb = e.astype(BF16).astype(F32)
@@ -339,88 +306,66 @@
         for r in range(group):
             b = base + r
             o = jnp.dot(es[r], v_s[b], preferred_element_type=F32) + news[r] * values[r]
-            at = pl.ds(pl.multiple_of(b * half_heads, 8), half_heads)
-            ost_s[0, at, :] = o[:half_heads]
-            ost_s[1, at, :] = o[half_heads:]
+            at = pl.ds(pl.multiple_of((b - h * hr) * half_heads, 8), half_heads)
+            ost_s[0, h, at, :] = o[:half_heads]
+            ost_s[1, h, at, :] = o[half_heads:]
         return mm, ll
 
-    ph('kv_wait')
-    for i in range(n_kv):
-        kv_copy(0, i).wait()
-        kv_copy(1, i).wait()
+    def attend_half(h):
+        zero = jnp.zeros((heads, seq), F32)
+        mm, ll = lax.fori_loop(2 * h, 2 * h + 2, functools.partial(attend, h), (zero, zero))
+        ml = jnp.concatenate([mm, ll], axis=-1)
+        ost_s[0, h, top_rows:, :] = ml[:half_heads]
+        ost_s[1, h, top_rows:, :] = ml[half_heads:]
+        st_copy(h).start()
+
     ph('attention')
-    zero = jnp.zeros((heads, seq), F32)
-    mm, ll = lax.fori_loop(0, 3, attend, (zero, zero))
-
-    ph('rs_sum')
-    for i in range(4, 8):
-        rs_copy(i).wait_recv()
-    ma_s[c * chips + z] = ss_s[7] + rb_s[0] + rb_s[1] + rb_s[2] + rb_s[3]
-    for i in range(4):
-        ma_copy(i).start()
-    ma_fwd(c, 0).start()
+    for i in range(n_up):
+        up_copy(i).start()
+    attend_half(0)
 
     ph('attention_last')
-    mm, ll = lax.fori_loop(3, 4, attend, (mm, ll))
-    ml = jnp.concatenate([mm, ll], axis=-1)
-    ost_s[0, rows * half_heads:, :] = ml[:half_heads]
-    ost_s[1, rows * half_heads:, :] = ml[half_heads:]
-    st_copy().start()
-
-    ph('stat_wait')
-    st_copy().wait_recv()
-    ph('merge')
-    base = rows * half_heads
-    m_s, l_s = ost_s[c, base:, :HALF], ost_s[c, base:, HALF:]
-    m_p, l_p = orx_s[base:, :HALF], orx_s[base:, HALF:]
-    m_c = jnp.maximum(m_s, m_p)
-    w_own, w_par = jnp.exp(m_s - m_c), jnp.exp(m_p - m_c)
-
-    def put(at, val):
-        cz_s[pl.ds(at, half_heads, stride=chunk), :] = val
-
-    for b in range(rows):
-        sl = slice(b * half_heads, (b + 1) * half_heads)
-        mix = ost_s[c, sl, :] * w_own[:, b:b + 1] + orx_s[sl, :] * w_par[:, b:b + 1]
-        at = b if b < hr else hi_at + b - hr
-        put(at, mix[:, :HALF])
-        put(at + hr, mix[:, HALF:])
-    put(ml_at, m_c)
-    put(ml_at + 1, l_s * w_own + l_p * w_par)
-    nil = jnp.zeros((half_heads, HALF), F32)
-    for i in range(2, 8):
-        put(ml_at + i, nil)
-    for i in (2, 3, 0, 1):
-        aa_copy(i).start()
-
-    row_lane = lax.broadcasted_iota(jnp.int32, (1, HALF), 1)
-    is_lo = row_lane < hr
-
-    def blend(parts, out):
-        ms, ls = [], []
-        for ref, at, lo, hi in parts:
-            m, l = ref[at:at + 1, :], ref[at + 1:at + 2, :]
-            if lo is None:
-                m, l = jnp.where(is_lo, NEG_FILL, m), jnp.where(is_lo, 0.0, l)
-            if hi is None:
-                m, l = jnp.where(is_lo, m, NEG_FILL), jnp.where(is_lo, l, 0.0)
-            ms.append(m)
-            ls.append(l)
+    attend_half(1)
+    for half in range(2):
+        for i in range(chips):
+            dn_copy(half, i).start()
+
+    def merge(h):
+        m_s, l_s = ost_s[c, h, top_rows:, :HALF], ost_s[c, h, top_rows:, HALF:]
+        m_p, l_p = orx_s[h, top_rows:, :HALF], orx_s[h, top_rows:, HALF:]
+        m_c = jnp.maximum(m_s, m_p)
+        w_own, w_par = jnp.exp(m_s - m_c), jnp.exp(m_p - m_c)
+
+        def put(at, val):
+            cz_s[pl.ds(h * chips * chunk + at, half_heads, stride=chunk), :] = val
+
+        for b in range(hr):
+            sl = slice(b * half_heads, (b + 1) * half_heads)
+            mix = ost_s[c, h, sl, :] * w_own[:, b:b + 1] + orx_s[h, sl, :] * w_par[:, b:b + 1]
+            put(b, mix[:, :HALF])
+            put(hr + b, mix[:, HALF:])
+        put(ml_at, m_c)
+        put(ml_at + 1, l_s * w_own + l_p * w_par)
+
+    def mlp_up(i):
+        up_copy(i).wait()
+        up_copy(i + 1).wait()
+        us = chunk_dots(h_s, [(i + j) * up_rows for j in range(2)], up_rows)
+        for j, u in enumerate(us):
+            g = 0.5 * u * (1.0 + lax.erf(u * (0.5 ** 0.5)))
+            act_s[:, (i + j) * BLK:(i + j + 1) * BLK] = g.astype(BF16)
+
+    def blend(refs, out):
+        ms = [ref[ml_at:ml_at + 1, :] for ref in refs]
+        ls = [ref[ml_at + 1:ml_at + 2, :] for ref in refs]
         top = functools.reduce(jnp.maximum, ms)
         ws = [jnp.exp(m - top) for m in ms]
         l_sum = functools.reduce(lambda a, b: a + b, [l * w for l, w in zip(ls, ws)])
-        pad = [jnp.zeros_like(top)] * (8 - len(parts) - 1)
-        cols = jnp.transpose(jnp.concatenate(ws + [l_sum] + pad, axis=0))
-        for half in range(2):
-            for t in range(2):
-                acc = None
-                for j, (ref, at, lo, hi) in enumerate(parts):
-                    off = (lo, hi)[half]
-                    if off is None:
-                        continue
-                    term = ref[off + t * hr:off + (t + 1) * hr, :] * cols[half * hr:(half + 1) * hr, j:j + 1]
-                    acc = term if acc is None else acc + term
-                out(half, t, acc, cols[half * hr:(half + 1) * hr, len(parts):len(parts) + 1])
+        pad = [jnp.zeros_like(top)] * (8 - len(refs) - 1)
+        cols = jnp.transpose(jnp.concatenate(ws + [l_sum] + pad, axis=0))[:hr]
+        for t in range(2):
+            terms = [ref[t * hr:(t + 1) * hr, :] * cols[:, j:j + 1] for j, ref in enumerate(refs)]
+            out(t, functools.reduce(lambda a, b: a + b, terms), cols[:, len(refs):len(refs) + 1])
         return top, l_sum
 
     slot_f = lax.broadcasted_iota(jnp.int32, (seq, HALF), 0).astype(F32)
@@ -434,49 +379,89 @@
                 sl = slice(t * HALF, (t + 1) * HALF)
                 ref[b, :, sl] = jnp.where(hit, new, ref[b, :, sl].astype(F32)).astype(BF16)
 
+    for h in range(2):
+        ph(f'stat_wait{h}')
+        st_copy(h).wait_recv()
+        ph(f'merge{h}')
+        merge(h)
+        for i in (2, 0, 1):
+            aa_copy(h, i).start()
+        ph(f'mlp_up{h}')
+        if h == 1:
+            for k in range(2):
+                for i in (5, 6):
+                    aa_copy(k, i).start()
+            for i in range(n_col // 2, n_col):
+                wo_copy(i).start()
+        mlp_up(h * n_up // 2)
+    ph('down_partner')
+    for i in range(0, chips, 4):
+        for j in range(4):
+            dn_copy(0, i + j).wait()
+        for j, p in enumerate(chunk_dots(act_s, [dn_base + (i + j) * dn_rows for j in range(4)], dn_rows)):
+            ps_s[i + j] = p
+            pd_copy(i + j).start()
+
+    ph('down_own')
+    for i in range(0, chips, 4):
+        for j in range(4):
+            dn_copy(1, i + j).wait()
+        for j, p in enumerate(chunk_dots(act_s, [dn_base + (chips + i + j) * dn_rows for j in range(4)], dn_rows)):
+            n = i + j
+            pd_copy(n).wait_recv()
+            ss_s[n] = p + pr_s[n]
+            for m in ((0,), (1,), (2, 3), (), (), (6,), (7,), ())[n]:
+                rs_copy(m).start()
+
+    for i in range(n_col // 2):
+        wo_copy(i).start()
+    for h in range(2):
+        ph(f'aa_wait{h}')
+        for i in range(3):
+            aa_copy(h, i).wait_recv()
+        ph(f'aa_add{h}')
+        for side in range(2):
+            def keep(t, acc, _):
+                tw_s[h, side, t * hr:(t + 1) * hr, :] = acc
+
+            more = [ta_s.at[h, 2]] if side == h else []
+            top, l_sum = blend([cz_at(h, (2, -2)[side]), ta_s.at[h, side]] + more, keep)
+            tw_s[h, side, ml_at:, :] = jnp.concatenate([top, l_sum, jnp.zeros((6, HALF), F32)], axis=0)
+            aa_copy(h, 3 + side).start()
     ph('insert_k')
     insert(k_s, heads)
-    ph('ma_on')
-    ma_wait(0)
-    ma_wait(1)
-    for i in range(4, 8):
-        ma_copy(i).start()
-    ma_wait(2)
-    ma_wait(3)
-    for k in (2, -2, 1, -1):
-        ma_fwd(c, k).start()
-
-    for i in (6, 7):
-        aa_copy(i).start()
-    ph('aa_wait')
+    ph('rs_add')
     for i in range(4):
-        aa_copy(i).wait_recv()
-    ph('aa_add')
-    for side, k in ((0, 2), (1, -2)):
-        half_part = (ta_s.at[2], ml_at, 0, None) if side == 0 else (ta_s.at[3], 0, None, 8)
-
-        def keep(half, t, acc, _, side=side):
-            off = (0, hi_at)[half] + t * hr
-            tw_s[side, off:off + hr, :] = acc
-
-        top, l_sum = blend([(cz_at(k, 0, chunk), ml_at, 0, hi_at), (ta_s.at[side], ml_at, 0, hi_at), half_part], keep)
-        tw_s[side, ml_at:ml_at + 8, :] = jnp.concatenate([top, l_sum, jnp.zeros((6, HALF), F32)], axis=0)
-        aa_copy(4 + side).start()
-
+        rs_copy(i).wait_recv()
+    ss_s[3, 0:hr] = ss_s[3, 0:hr] + ra_s[0, 0:hr] + ra_s[2, 0:hr]
+    ss_s[3, hr:] = ss_s[3, hr:] + ra_s[0, hr:]
+    ss_s[4, 0:hr] = ss_s[4, 0:hr] + ra_s[1, 0:hr]
+    ss_s[4, hr:] = ss_s[4, hr:] + ra_s[1, hr:] + ra_s[2, hr:]
+    rs_copy(4).start()
+    rs_copy(5).start()
     ph('insert_v')
     insert(v_s, heads + 1)
-    ph('aa_wait2')
+    for h in range(2):
+        ph(f'aa_last{h}')
+        for i in range(3, 7):
+            aa_copy(h, i).wait_recv()
+        ph(f'context{h}')
+
+        def finish(t, acc, l_col):
+            g_s[c * chips + z, h * hr:(h + 1) * hr, t * HALF:(t + 1) * HALF] = (acc / l_col).astype(BF16).astype(F32)
+
+        blend([cz_at(h, 0)] + [tb_s.at[h, j] for j in range(4)], finish)
+        for i in range(4):
+            cg_copy(h, i).start()
+    cg_fwd(c, 0).start()
+
+    ph('rs_sum')
     for i in range(4, 8):
-        aa_copy(i).wait_recv()
-    ph('context')
-
-    def finish(half, t, acc, l_col):
-        g_s[c * chips + z, half * hr:(half + 1) * hr, t * HALF:(t + 1) * HALF] = (acc / l_col).astype(BF16).astype(F32)
-
-    blend([(cz_at(0, 0, chunk), ml_at, 0, hi_at)] + [(tb_s.at[j], ml_at, 0, hi_at) for j in range(4)], finish)
+        rs_copy(i).wait_recv()
+    ma_s[c * chips + z] = ss_s[7] + rb_s[0] + rb_s[1] + rb_s[2] + rb_s[3]
     for i in range(4):
-        cg_copy(i).start()
-    cg_fwd(c, 0).start()
+        ma_copy(i).start()
+    ma_fwd(c, 0).start()
 
     ph('wo_wait')
     for i in range(n_col):
@@ -506,45 +491,62 @@
     ph('out_0b')
     out_dots([theirs(0)])
     ph('cg_wait1')
-    cg_wait(0)
-    cg_copy(6).start()
-    cg_copy(4).start()
-    cg_wait(1)
-    cg_copy(7).start()
-    cg_copy(5).start()
+    for h in range(2):
+        cg_wait(h, 0)
+        if h == 0:
+            cg_copy(0, 6).start()
+        cg_copy(h, 4).start()
+        cg_wait(h, 1)
+        if h == 1:
+            cg_copy(1, 6).start()
+        cg_copy(h, 5).start()
     cg_fwd(c, -2).start()
     cg_fwd(c, 2).start()
-    cg_wait(2)
+    cg_wait(0, 2)
+    cg_wait(1, 2)
     cg_fwd(c, -1).start()
-    cg_wait(3)
+    cg_wait(0, 3)
+    cg_wait(1, 3)
     cg_fwd(c, 1).start()
     ph('out_1')
     out_dots([mine(-2), mine(2), mine(-1), mine(1)])
-    ph('ma_tail')
+    ph('ma_on')
+    ma_wait(0)
+    ma_wait(1)
     for i in range(4, 8):
-        ma_wait(i)
-    for k in (3, -3, 4):
+        ma_copy(i).start()
+    ma_wait(2)
+    ma_wait(3)
+    for k in (2, -2, 1, -1):
         ma_fwd(c, k).start()
+
     ph('cg_wait2')
     for k in (-2, 2, -1, 1):
         cg_fwd(pc, k).wait_recv()
     ph('out_2')
     out_dots([theirs(-2), theirs(2), theirs(-1), theirs(1)])
     ph('cg_wait3')
-    cg_wait(4)
+    cg_wait(0, 4)
+    cg_wait(1, 4)
     cg_fwd(c, -3).start()
-    cg_wait(5)
+    cg_wait(0, 5)
+    cg_wait(1, 5)
     cg_fwd(c, 3).start()
     ph('out_3')
     out_dots([mine(-3), mine(3)])
     ph('cg_wait4')
-    cg_wait(6)
-    cg_wait(7)
+    cg_wait(0, 6)
+    cg_wait(1, 6)
     cg_fwd(c, 4).start()
     cg_fwd(pc, -3).wait_recv()
     cg_fwd(pc, 3).wait_recv()
     ph('out_4')
     out_dots([mine(4), theirs(-3), theirs(3)])
+    ph('ma_tail')
+    for i in range(4, 8):
+        ma_wait(i)
+    for k in (3, -3, 4):
+        ma_fwd(c, k).start()
     ph('cg_wait5')
     cg_fwd(pc, 4).wait_recv()
     ph('out_5')
@@ -563,12 +565,14 @@
         cg_fwd(c, i).wait_send()
     for i in range(8):
         rs_copy(i).wait_send()
-        aa_copy(i).wait_send()
         ma_copy(i).wait_send()
-        cg_copy(i).wait_send()
+    for h in range(2):
+        st_copy(h).wait_send()
+        for i in range(7):
+            aa_copy(h, i).wait_send()
+            cg_copy(h, i).wait_send()
     for i in range(slots):
         qx_copy(c, i).wait_send()
-    st_copy().wait_send()
     ph(None)
 
 
@@ -598,13 +602,13 @@
     inv_freq = 1.0 / (ROPE_BASE ** (jnp.arange(0, head_dim, 2, dtype=F32) / head_dim))
     n_up, n_col = ff // BLK, d_model // BLK
     w_rows = n_up * d_model + n_col * ff + slots * d_model
-    n_kv = 3
+    n_kv = 4
     half = heads // 2
     any_spec = pl.BlockSpec(memory_space=pltpu.HBM)
     vmem_spec = pl.BlockSpec(memory_space=pltpu.VMEM)
     dma = pltpu.SemaphoreType.DMA
     hr = rows // 2
-    chunk, part = 4 * hr + 8, 2 * hr + 8
+    chunk = 2 * hr + 8
     scratch = [
         pltpu.VMEM((rows, d_model), BF16),
         pltpu.VMEM((16, d_model), F32),
@@ -622,17 +626,17 @@
         pltpu.VMEM((3, rows, BLK), F32),
         pltpu.VMEM((4, rows, BLK), F32),
         pltpu.VMEM((n_sp, rows, BLK), F32),
-        pltpu.VMEM((2, (rows + 1) * half, BLK), F32),
-        pltpu.VMEM(((rows + 1) * half, BLK), F32),
-        pltpu.VMEM((chips * chunk, HALF), F32),
-        pltpu.VMEM((4, chunk, HALF), F32),
-        pltpu.VMEM((4, chunk, HALF), F32),
-        pltpu.VMEM((2, chunk, HALF), F32),
+        pltpu.VMEM((2, 2, (hr + 1) * half, BLK), F32),
+        pltpu.VMEM((2, (hr + 1) * half, BLK), F32),
+        pltpu.VMEM((2 * chips * chunk, HALF), F32),
+        pltpu.VMEM((2, 3, chunk, HALF), F32),
+        pltpu.VMEM((2, 4, chunk, HALF), F32),
+        pltpu.VMEM((2, 2, chunk, HALF), F32),
         pltpu.VMEM((n_sp, rows, BLK), F32),
         pltpu.VMEM((rows, d_model), F32),
         dma((4,)), dma((n_up,)), dma((n_col,)), dma((slots,)), dma((2, n_kv)), dma((n_col,)),
-        dma((chips,)), dma((chips,)), dma((slots,)), dma((slots,)), dma((1,)), dma((1,)),
-    ] + [dma((8,))] * 12
+        dma((chips,)), dma((chips,)), dma((slots,)), dma((slots,)), dma((2,)), dma((2,)),
+    ] + [dma((n,)) for n in (8, 8, 14, 14, 8, 8, 8, 8, 14, 14, 8, 8)]
     in_hbm = [pltpu.with_memory_space_constraint(a, pltpu.HBM) for a in (hidden, ln_gamma.reshape(1, -1), ln_beta.reshape(1, -1))]
     results = pl.pallas_call(
         functools.partial(layer_kernel, chips, heads),

time: 53.6 us -> 50.2 us (0.937)
  Pallas kernels: 52.8 us -> 49.3 us
    pallas_call x1, Pallas kernels: 50 us -> 46.4 us  [device_step(): pl.pallas_call(functools.partial(layer_kernel, chips, heads), out_shape=(...]
where the time goes in v4:
time: 50.2 us; the launch traced here: 50.1 us
  Pallas kernels  49.3 us (98%)
  between operations  0.8 us (2%)
    pallas_call x1, Pallas kernels, device_step(): pl.pallas_call(functools.partial(layer_kernel, chips, heads), out_shape=(...  46.4 us
    pallas_call x1, Pallas kernels, device_step(): pl.pallas_call(store_kernel, out_shape=[jax.ShapeDtypeStruct(r.shape, r.d...  2.88 us

profile of v4, /device:TPU:21, one launch (start us, length us, event | category | flops | bytes accessed | tf_op | source)
XLA Modules:
  0.0 50.1 jit_solution(13187870320222431402)
XLA Ops:
  0.6 46.4 %decode_layer.1 = (bf16[48,4096]{1,0:T(8,128)(2,1)S(1)}, bf16[48,128,256]{2,1,0:T(8,128)(2,1)S(1)}, bf16[48,128,256]{2,1,0:T(8,128)(2,1)S(1)}) custom-call(bf16[48,4096]{1,0:T(8,128)(2,1)} %x_hbm.1, f32[1,4096]{1,0:T(1,128)} %bitcast.2, f32[1,4096]{1,0:T(1,128)} %bitcast.3, bf16[4096,4608]{1,0:T(8,128)(2,1)} %wqkv_hbm.1, bf16[4096,4096]{1,0:T(8,128)(2,1)} %wout_hbm.1, ...), custom_call_target="tpu_custom_call" | custom-call | tf_op jit(solution)/shard_map/decode_layer/pallas_call | solution.py:641
  47.1 2.9 %store_results.1 = (bf16[48,4096]{1,0:T(8,128)(2,1)}, bf16[48,128,256]{2,1,0:T(8,128)(2,1)}, bf16[48,128,256]{2,1,0:T(8,128)(2,1)}) custom-call(bf16[48,4096]{1,0:T(8,128)(2,1)S(1)} %get-tuple-element.6.refs_0_, bf16[48,128,256]{2,1,0:T(8,128)(2,1)S(1)} %get-tuple-element.7.refs_1_, bf16[48,128,256]{2,1,0:T(8,128)(2,1)S(1)} %get-tuple-element.8.refs_2_), custom_call_target="tpu_custom_call" | custom-call | tf_op jit(solution)/shard_map/store_results/pallas_call | solution.py:650
  (1 shorter events, 0.0 us)

commit v5 on v4

--- a/solution.py
+++ b/solution.py
@@ -13,6 +13,7 @@
 MESH = pl.DeviceIdType.MESH
 BLK = 256
 HALF = 128
+SIDES = range(2)
 F32 = jnp.float32
 BF16 = jnp.bfloat16
 
@@ -49,6 +50,7 @@
     hr = rows // 2
     ml_at = 2 * hr
     chunk = 2 * hr + 8
+    used = 2 * hr + 2
     top_rows = hr * half_heads
     up_rows, dn_rows = d_model, ff
     dn_base = n_up * up_rows
@@ -113,58 +115,55 @@
     def st_copy(h):
         return remote(ost_s.at[pc, h], orx_s.at[h], st_send.at[h], st_recv.at[h], partner)
 
-    hops = (1, -1, 2, -2, 2, -2, 1, -1)
-
-    def rs_copy(i):
-        src = (ss_s.at[0], ss_s.at[1], ss_s.at[2, pl.ds(0, hr)], ss_s.at[2, pl.ds(hr, hr)], ss_s.at[3], ss_s.at[4], ss_s.at[5], ss_s.at[6])[i]
-        dst = (ra_s.at[0], ra_s.at[1], ra_s.at[2, pl.ds(0, hr)], ra_s.at[2, pl.ds(hr, hr)], rb_s.at[0], rb_s.at[1], rb_s.at[2], rb_s.at[3])[i]
-        return remote(src, dst, rs_send.at[i], rs_recv.at[i], peer(hops[i]))
-
-    def cz_at(h, k):
-        return cz_s.at[pl.ds(pl.multiple_of((h * chips + chip(k)) * chunk, 8), chunk)]
-
-    def aa_copy(h, i):
-        src = (lambda: cz_at(h, 3), lambda: cz_at(h, -3), lambda: cz_at(h, 4), lambda: tw_s.at[h, 0], lambda: tw_s.at[h, 1],
-               lambda: cz_at(h, 1), lambda: cz_at(h, -1))[i]()
-        dst = ta_s.at[h, i] if i < 3 else tb_s.at[h, i - 3]
-        hop = (1, -1, (2, -2)[h], 2, -2, 1, -1)[i]
-        return remote(src, dst, aa_send.at[7 * h + i], aa_recv.at[7 * h + i], peer(hop))
-
-    g_hop = (2, -2, 1, -1, 1, -1, 2, -2)
-    g_src = (0, 0, 0, 0, -2, 2, -2, 2)
-
-    def gather_copy(buf, send, recv, i):
-        ref = buf.at[c * chips + chip(g_src[i])]
-        if i >= 6:
-            ref = ref.at[pl.ds((i - 6) * hr, hr)]
-        return remote(ref, ref, send.at[i], recv.at[i], peer(g_hop[i]))
-
-    def gather_recv(buf, send, recv, i):
-        ref = buf.at[c * chips + chip(g_src[i] - g_hop[i])]
-        if i >= 6:
-            ref = ref.at[pl.ds((i - 6) * hr, hr)]
-        return remote(ref, ref, send.at[i], recv.at[i], peer(g_hop[i]))
-
-    def ma_copy(i):
-        return gather_copy(ma_s, ma_send, ma_recv, i)
-
-    def cg_route(h, i):
-        return ((0, 2), (0, -2), (0, 1), (0, -1), (-2, 1), (2, -1), ((-2, 2), (2, -2))[h])[i]
-
-    def cg_part(h, i, k, hop):
-        ref = g_s.at[c * chips + chip(k), pl.ds(h * hr, hr)]
-        return remote(ref, ref, cg_send.at[7 * h + i], cg_recv.at[7 * h + i], peer(hop))
-
-    def cg_copy(h, i):
-        src, hop = cg_route(h, i)
-        return cg_part(h, i, src, hop)
-
-    def ma_wait(i):
-        gather_recv(ma_s, ma_send, ma_recv, i).wait_recv()
-
-    def cg_wait(h, i):
-        src, hop = cg_route(h, i)
-        cg_part(h, i, src - hop, hop).wait_recv()
+    def sign(side):
+        return 1 - 2 * side
+
+    def rows_of(side):
+        return pl.ds(side * hr, hr)
+
+    def rs_copy(kind, side):
+        src = (ss_s.at[side], ss_s.at[2, rows_of(side)], ss_s.at[3 + side], ss_s.at[5 + side])[kind]
+        dst = (ra_s.at[side], ra_s.at[2, rows_of(side)], rb_s.at[side], rb_s.at[2 + side])[kind]
+        at = 2 * kind + side
+        return remote(src, dst, rs_send.at[at], rs_recv.at[at], peer(sign(side) * (1 if kind in (0, 3) else 2)))
+
+    def cz_at(h, k, n=chunk):
+        return cz_s.at[pl.ds(pl.multiple_of((h * chips + chip(k)) * chunk, 8), n)]
+
+    def aa_copy(h, kind, side):
+        sg, rows_used = sign(side), pl.ds(0, used)
+        src = tw_s.at[h, side, rows_used] if kind == 2 else cz_at(h, sg * (3, 4, 2, 1)[kind], used)
+        dst = (ta_s.at[h, side], ta_s.at[h, 2], tb_s.at[h, side], tb_s.at[h, 2 + side])[kind].at[rows_used]
+        at = 8 * h + 2 * kind + side
+        return remote(src, dst, aa_send.at[at], aa_recv.at[at], peer(sg * (1 if kind in (0, 3) else 2)))
+
+    def route(kind, side):
+        return [sign(side) * v for v in ((0, 2), (0, 1), (-2, 1), (-2, 2))[kind]]
+
+    def ma_part(kind, side, k, hop):
+        ref = ma_s.at[c * chips + chip(k)]
+        ref = ref.at[rows_of(side)] if kind == 3 else ref
+        at = 2 * kind + side
+        return remote(ref, ref, ma_send.at[at], ma_recv.at[at], peer(hop))
+
+    def ma_copy(kind, side):
+        return ma_part(kind, side, *route(kind, side))
+
+    def ma_wait(kind, side):
+        src, hop = route(kind, side)
+        ma_part(kind, side, src - hop, hop).wait_recv()
+
+    def cg_part(h, kind, side, k, hop):
+        ref = g_s.at[c * chips + chip(k), rows_of(h)]
+        at = 8 * h + 2 * kind + side
+        return remote(ref, ref, cg_send.at[at], cg_recv.at[at], peer(hop))
+
+    def cg_copy(h, kind, side):
+        return cg_part(h, kind, side, *route(kind, side))
+
+    def cg_wait(h, kind, side):
+        src, hop = route(kind, side)
+        cg_part(h, kind, side, src - hop, hop).wait_recv()
 
     def ma_fwd(owner, k):
         ref = ma_s.at[owner * chips + chip(k)]
@@ -188,7 +187,7 @@
     ph('in_wait')
     for i in range(4):
         in_copy(i).wait()
-    for i in range(2, slots):
+    for i in range(2, 5):
         qkv_copy(i).start()
     ph('layer_norm')
 
@@ -201,9 +200,10 @@
         var = jnp.mean(cen * cen, axis=-1, keepdims=True)
         h_s[sl, :] = (cen * lax.rsqrt(var + LN_EPS) * gb_s[0:1, :] + gb_s[8:9, :]).astype(BF16)
 
+    qkv_copy(5).start()
     nil = jnp.zeros((half_heads, HALF), F32)
     for h in range(2):
-        for i in range(ml_at + 2, chunk):
+        for i in range(used, chunk):
             cz_s[pl.ds(h * chips * chunk + i, half_heads, stride=chunk), :] = nil
     ph('rope')
     for b in range(rows):
@@ -246,6 +246,8 @@
     n_pair = slots // 2
     ph('qkv')
     qkv_pair(0, False)
+    for i in range(6, slots):
+        qkv_copy(i).start()
     ph('barrier')
     pl.semaphore_wait(bar, 5)
     ph('qkv2')
@@ -384,13 +386,14 @@
         st_copy(h).wait_recv()
         ph(f'merge{h}')
         merge(h)
-        for i in (2, 0, 1):
-            aa_copy(h, i).start()
+        aa_copy(h, 1, h).start()
+        for side in SIDES:
+            aa_copy(h, 0, side).start()
         ph(f'mlp_up{h}')
         if h == 1:
             for k in range(2):
-                for i in (5, 6):
-                    aa_copy(k, i).start()
+                for side in SIDES:
+                    aa_copy(k, 3, side).start()
             for i in range(n_col // 2, n_col):
                 wo_copy(i).start()
         mlp_up(h * n_up // 2)
@@ -410,59 +413,56 @@
             n = i + j
             pd_copy(n).wait_recv()
             ss_s[n] = p + pr_s[n]
-            for m in ((0,), (1,), (2, 3), (), (), (6,), (7,), ())[n]:
-                rs_copy(m).start()
-
+            if n < 2:
+                rs_copy(0, n).start()
+            elif n == 2:
+                for side in SIDES:
+                    rs_copy(1, side).start()
+
+    for side in SIDES:
+        rs_copy(3, side).start()
     for i in range(n_col // 2):
         wo_copy(i).start()
     for h in range(2):
         ph(f'aa_wait{h}')
-        for i in range(3):
-            aa_copy(h, i).wait_recv()
+        aa_copy(h, 1, h).wait_recv()
+        for side in SIDES:
+            aa_copy(h, 0, side).wait_recv()
         ph(f'aa_add{h}')
         for side in range(2):
             def keep(t, acc, _):
                 tw_s[h, side, t * hr:(t + 1) * hr, :] = acc
 
             more = [ta_s.at[h, 2]] if side == h else []
-            top, l_sum = blend([cz_at(h, (2, -2)[side]), ta_s.at[h, side]] + more, keep)
+            top, l_sum = blend([cz_at(h, sign(side) * 2), ta_s.at[h, side]] + more, keep)
             tw_s[h, side, ml_at:, :] = jnp.concatenate([top, l_sum, jnp.zeros((6, HALF), F32)], axis=0)
-            aa_copy(h, 3 + side).start()
+            aa_copy(h, 2, side).start()
     ph('insert_k')
     insert(k_s, heads)
-    ph('rs_add')
-    for i in range(4):
-        rs_copy(i).wait_recv()
-    ss_s[3, 0:hr] = ss_s[3, 0:hr] + ra_s[0, 0:hr] + ra_s[2, 0:hr]
-    ss_s[3, hr:] = ss_s[3, hr:] + ra_s[0, hr:]
-    ss_s[4, 0:hr] = ss_s[4, 0:hr] + ra_s[1, 0:hr]
-    ss_s[4, hr:] = ss_s[4, hr:] + ra_s[1, hr:] + ra_s[2, hr:]
-    rs_copy(4).start()
-    rs_copy(5).start()
     ph('insert_v')
     insert(v_s, heads + 1)
+    ph('rs_add')
+    for side in SIDES:
+        rs_copy(0, side).wait_recv()
+        rs_copy(1, side).wait_recv()
+        ss_s[3 + side] = ss_s[3 + side] + ra_s[side]
+        ss_s[3 + side, rows_of(side)] = ss_s[3 + side, rows_of(side)] + ra_s[2, rows_of(side)]
+        rs_copy(2, side).start()
     for h in range(2):
         ph(f'aa_last{h}')
-        for i in range(3, 7):
-            aa_copy(h, i).wait_recv()
+        for side in SIDES:
+            aa_copy(h, 2, side).wait_recv()
+            aa_copy(h, 3, side).wait_recv()
         ph(f'context{h}')
 
         def finish(t, acc, l_col):
             g_s[c * chips + z, h * hr:(h + 1) * hr, t * HALF:(t + 1) * HALF] = (acc / l_col).astype(BF16).astype(F32)
 
         blend([cz_at(h, 0)] + [tb_s.at[h, j] for j in range(4)], finish)
-        for i in range(4):
-            cg_copy(h, i).start()
+        for kind in range(2):
+            for side in SIDES:
+                cg_copy(h, kind, side).start()
     cg_fwd(c, 0).start()
-
-    ph('rs_sum')
-    for i in range(4, 8):
-        rs_copy(i).wait_recv()
-    ma_s[c * chips + z] = ss_s[7] + rb_s[0] + rb_s[1] + rb_s[2] + rb_s[3]
-    for i in range(4):
-        ma_copy(i).start()
-    ma_fwd(c, 0).start()
-
     ph('wo_wait')
     for i in range(n_col):
         wo_copy(i).wait()
@@ -490,35 +490,40 @@
     cg_fwd(pc, 0).wait_recv()
     ph('out_0b')
     out_dots([theirs(0)])
+    ph('rs_sum')
+    for side in SIDES:
+        rs_copy(2, side).wait_recv()
+        rs_copy(3, side).wait_recv()
+    ma_s[c * chips + z] = ss_s[7] + rb_s[0] + rb_s[1] + rb_s[2] + rb_s[3]
+    for kind in range(2):
+        for side in SIDES:
+            ma_copy(kind, side).start()
+    ma_fwd(c, 0).start()
+
     ph('cg_wait1')
     for h in range(2):
-        cg_wait(h, 0)
-        if h == 0:
-            cg_copy(0, 6).start()
-        cg_copy(h, 4).start()
-        cg_wait(h, 1)
-        if h == 1:
-            cg_copy(1, 6).start()
-        cg_copy(h, 5).start()
-    cg_fwd(c, -2).start()
-    cg_fwd(c, 2).start()
-    cg_wait(0, 2)
-    cg_wait(1, 2)
-    cg_fwd(c, -1).start()
-    cg_wait(0, 3)
-    cg_wait(1, 3)
-    cg_fwd(c, 1).start()
+        for side in SIDES:
+            cg_wait(h, 0, side)
+            if h == side:
+                cg_copy(h, 3, side).start()
+            cg_copy(h, 2, side).start()
+    for k in (-2, 2):
+        cg_fwd(c, k).start()
+    for side in SIDES:
+        for h in range(2):
+            cg_wait(h, 1, side)
+        cg_fwd(c, -sign(side)).start()
     ph('out_1')
     out_dots([mine(-2), mine(2), mine(-1), mine(1)])
     ph('ma_on')
-    ma_wait(0)
-    ma_wait(1)
-    for i in range(4, 8):
-        ma_copy(i).start()
-    ma_wait(2)
-    ma_wait(3)
-    for k in (2, -2, 1, -1):
-        ma_fwd(c, k).start()
+    for side in SIDES:
+        ma_wait(0, side)
+        ma_copy(3, side).start()
+        ma_copy(2, side).start()
+        ma_fwd(c, -2 * sign(side)).start()
+    for side in SIDES:
+        ma_wait(1, side)
+        ma_fwd(c, -sign(side)).start()
 
     ph('cg_wait2')
     for k in (-2, 2, -1, 1):
@@ -526,27 +531,26 @@
     ph('out_2')
     out_dots([theirs(-2), theirs(2), theirs(-1), theirs(1)])
     ph('cg_wait3')
-    cg_wait(0, 4)
-    cg_wait(1, 4)
-    cg_fwd(c, -3).start()
-    cg_wait(0, 5)
-    cg_wait(1, 5)
-    cg_fwd(c, 3).start()
+    for side in SIDES:
+        for h in range(2):
+            cg_wait(h, 2, side)
+        cg_fwd(c, -3 * sign(side)).start()
     ph('out_3')
     out_dots([mine(-3), mine(3)])
     ph('cg_wait4')
-    cg_wait(0, 6)
-    cg_wait(1, 6)
+    for side in SIDES:
+        cg_wait(side, 3, side)
     cg_fwd(c, 4).start()
     cg_fwd(pc, -3).wait_recv()
     cg_fwd(pc, 3).wait_recv()
     ph('out_4')
     out_dots([mine(4), theirs(-3), theirs(3)])
     ph('ma_tail')
-    for i in range(4, 8):
-        ma_wait(i)
-    for k in (3, -3, 4):
-        ma_fwd(c, k).start()
+    for side in SIDES:
+        ma_wait(2, side)
+        ma_wait(3, side)
+        ma_fwd(c, -3 * sign(side)).start()
+    ma_fwd(c, 4).start()
     ph('cg_wait5')
     cg_fwd(pc, 4).wait_recv()
     ph('out_5')
@@ -563,14 +567,17 @@
         pd_copy(i).wait_send()
         ma_fwd(c, i).wait_send()
         cg_fwd(c, i).wait_send()
-    for i in range(8):
-        rs_copy(i).wait_send()
-        ma_copy(i).wait_send()
     for h in range(2):
         st_copy(h).wait_send()
-        for i in range(7):
-            aa_copy(h, i).wait_send()
-            cg_copy(h, i).wait_send()
+    for kind in range(4):
+        for side in SIDES:
+            rs_copy(kind, side).wait_send()
+            ma_copy(kind, side).wait_send()
+            for h in range(2):
+                if (h == side) or kind != 1:
+                    aa_copy(h, kind, side).wait_send()
+                if (h == side) or kind < 3:
+                    cg_copy(h, kind, side).wait_send()
     for i in range(slots):
         qx_copy(c, i).wait_send()
     ph(None)
@@ -636,7 +643,7 @@
         pltpu.VMEM((rows, d_model), F32),
         dma((4,)), dma((n_up,)), dma((n_col,)), dma((slots,)), dma((2, n_kv)), dma((n_col,)),
         dma((chips,)), dma((chips,)), dma((slots,)), dma((slots,)), dma((2,)), dma((2,)),
-    ] + [dma((n,)) for n in (8, 8, 14, 14, 8, 8, 8, 8, 14, 14, 8, 8)]
+    ] + [dma((n_sp,))] * 12
     in_hbm = [pltpu.with_memory_space_constraint(a, pltpu.HBM) for a in (hidden, ln_gamma.reshape(1, -1), ln_beta.reshape(1, -1))]
     results = pl.pallas_call(
         functools.partial(layer_kernel, chips, heads),
@@ -659,7 +666,7 @@
 
 
 def solution(mesh):
-    cache_spec = P('dp', 'sp', None)
-    in_specs = (P('dp', None), P(None), P(None), P(None, None), P(None, None), P(None, 'sp'), P('sp', None), cache_spec, cache_spec, P('dp'))
-    out_specs = (P('dp', None), cache_spec, cache_spec)
+    rows, cache = P('dp'), P('dp', 'sp')
+    in_specs = (rows, P(), P(), P(), P(), P(None, 'sp'), P('sp'), cache, cache, rows)
+    out_specs = (rows, cache, cache)
     return jax.shard_map(functools.partial(device_step, mesh.shape['sp']), mesh=mesh, in_specs=in_specs, out_specs=out_specs, check_vma=False)

time: 50.2 us -> 50.6 us (level)
  no operation moved by 1% of the time
where the time goes in v5:
time: 50.6 us; the launch traced here: 50.5 us
  Pallas kernels  49.7 us (98%)
  between operations  0.8 us (2%)
    pallas_call x1, Pallas kernels, device_step(): pl.pallas_call(functools.partial(layer_kernel, chips, heads), out_shape=(...  46.8 us
    pallas_call x1, Pallas kernels, device_step(): pl.pallas_call(store_kernel, out_shape=[jax.ShapeDtypeStruct(r.shape, r.d...  2.88 us

profile of v5, /device:TPU:21, one launch (start us, length us, event | category | flops | bytes accessed | tf_op | source)
XLA Modules:
  0.0 50.5 jit_solution(3916470515353629102)
XLA Ops:
  0.6 46.8 %decode_layer.1 = (bf16[48,4096]{1,0:T(8,128)(2,1)S(1)}, bf16[48,128,256]{2,1,0:T(8,128)(2,1)S(1)}, bf16[48,128,256]{2,1,0:T(8,128)(2,1)S(1)}) custom-call(bf16[48,4096]{1,0:T(8,128)(2,1)} %x_hbm.1, f32[1,4096]{1,0:T(1,128)} %bitcast.2, f32[1,4096]{1,0:T(1,128)} %bitcast.3, bf16[4096,4608]{1,0:T(8,128)(2,1)} %wqkv_hbm.1, bf16[4096,4096]{1,0:T(8,128)(2,1)} %wout_hbm.1, ...), custom_call_target="tpu_custom_call" | custom-call | tf_op jit(solution)/shard_map/decode_layer/pallas_call | solution.py:648
  47.5 2.9 %store_results.1 = (bf16[48,4096]{1,0:T(8,128)(2,1)}, bf16[48,128,256]{2,1,0:T(8,128)(2,1)}, bf16[48,128,256]{2,1,0:T(8,128)(2,1)}) custom-call(bf16[48,4096]{1,0:T(8,128)(2,1)S(1)} %get-tuple-element.6.refs_0_, bf16[48,128,256]{2,1,0:T(8,128)(2,1)S(1)} %get-tuple-element.7.refs_1_, bf16[48,128,256]{2,1,0:T(8,128)(2,1)S(1)} %get-tuple-element.8.refs_2_), custom_call_target="tpu_custom_call" | custom-call | tf_op jit(solution)/shard_map/store_results/pallas_call | solution.py:657
  (1 shorter events, 0.0 us)

commit v6 on v4

--- a/solution.py
+++ b/solution.py
@@ -176,7 +176,8 @@
 
     ph = Phases()
     ph('entry')
-    for i in range(4):
+    inputs = range(4)
+    for i in inputs:
         in_copy(i).start()
     for i in range(2):
         qkv_copy(i).start()
@@ -186,7 +187,7 @@
         pl.semaphore_signal(bar, inc=1, device_id=peer(k), device_id_type=MESH)
 
     ph('in_wait')
-    for i in range(4):
+    for i in inputs:
         in_copy(i).wait()
     for i in range(2, slots):
         qkv_copy(i).start()
@@ -636,7 +637,7 @@
         pltpu.VMEM((rows, d_model), F32),
         dma((4,)), dma((n_up,)), dma((n_col,)), dma((slots,)), dma((2, n_kv)), dma((n_col,)),
         dma((chips,)), dma((chips,)), dma((slots,)), dma((slots,)), dma((2,)), dma((2,)),
-    ] + [dma((n,)) for n in (8, 8, 14, 14, 8, 8, 8, 8, 14, 14, 8, 8)]
+    ] + [dma((n_sp,))] * 12
     in_hbm = [pltpu.with_memory_space_constraint(a, pltpu.HBM) for a in (hidden, ln_gamma.reshape(1, -1), ln_beta.reshape(1, -1))]
     results = pl.pallas_call(
         functools.partial(layer_kernel, chips, heads),
@@ -659,7 +660,7 @@
 
 
 def solution(mesh):
-    cache_spec = P('dp', 'sp', None)
-    in_specs = (P('dp', None), P(None), P(None), P(None, None), P(None, None), P(None, 'sp'), P('sp', None), cache_spec, cache_spec, P('dp'))
-    out_specs = (P('dp', None), cache_spec, cache_spec)
+    rows, cache = P('dp'), P('dp', 'sp')
+    in_specs = (rows, P(), P(), P(), P(), P(None, 'sp'), P('sp'), cache, cache, rows)
+    out_specs = (rows, cache, cache)
     return jax.shard_map(functools.partial(device_step, mesh.shape['sp']), mesh=mesh, in_specs=in_specs, out_specs=out_specs, check_vma=False)

time: 50.2 us -> 50.9 us (1.014)
  Pallas kernels: 49.3 us -> 50 us
    pallas_call x1, Pallas kernels: 46.4 us -> 47.1 us  [device_step(): pl.pallas_call(functools.partial(layer_kernel, chips, heads), out_shape=(...]
where the time goes in v6:
time: 50.9 us; the launch traced here: 50.8 us
  Pallas kernels  50 us (98%)
  between operations  0.8 us (2%)
    pallas_call x1, Pallas kernels, device_step(): pl.pallas_call(functools.partial(layer_kernel, chips, heads), out_shape=(...  47.1 us
    pallas_call x1, Pallas kernels, device_step(): pl.pallas_call(store_kernel, out_shape=[jax.ShapeDtypeStruct(r.shape, r.d...  2.88 us

profile of v6, /device:TPU:21, one launch (start us, length us, event | category | flops | bytes accessed | tf_op | source)
XLA Modules:
  0.0 50.8 jit_solution(10620920151601028715)
XLA Ops:
  0.6 47.1 %decode_layer.1 = (bf16[48,4096]{1,0:T(8,128)(2,1)S(1)}, bf16[48,128,256]{2,1,0:T(8,128)(2,1)S(1)}, bf16[48,128,256]{2,1,0:T(8,128)(2,1)S(1)}) custom-call(bf16[48,4096]{1,0:T(8,128)(2,1)} %x_hbm.1, f32[1,4096]{1,0:T(1,128)} %bitcast.2, f32[1,4096]{1,0:T(1,128)} %bitcast.3, bf16[4096,4608]{1,0:T(8,128)(2,1)} %wqkv_hbm.1, bf16[4096,4096]{1,0:T(8,128)(2,1)} %wout_hbm.1, ...), custom_call_target="tpu_custom_call" | custom-call | tf_op jit(solution)/shard_map/decode_layer/pallas_call | solution.py:642
  47.7 2.9 %store_results.1 = (bf16[48,4096]{1,0:T(8,128)(2,1)}, bf16[48,128,256]{2,1,0:T(8,128)(2,1)}, bf16[48,128,256]{2,1,0:T(8,128)(2,1)}) custom-call(bf16[48,4096]{1,0:T(8,128)(2,1)S(1)} %get-tuple-element.6.refs_0_, bf16[48,128,256]{2,1,0:T(8,128)(2,1)S(1)} %get-tuple-element.7.refs_1_, bf16[48,128,256]{2,1,0:T(8,128)(2,1)S(1)} %get-tuple-element.8.refs_2_), custom_call_target="tpu_custom_call" | custom-call | tf_op jit(solution)/shard_map/store_results/pallas_call | solution.py:651
  (1 shorter events, 0.0 us)
